TPU v7x, 512 devices: a 4x2x32 block of a 4x8x32 slice. The times are simulated.
512 devices in a mesh: cfg: 2 (over y), expert: 64 (over z, core), ffn: 4 (over x).
Axes of the slice: x: 4, y: 2, z: 32, core: 2. Of those that a mesh axis runs over, the one named last changes fastest.
The devices are a block of a 4x8x32 slice.
Arguments:
- tokens: bfloat16 [32768, 2048], P(('cfg', 'expert'), 'ffn'), parts along dimension 0, may hold values from -6 to 6
- chosen: int32 [128, 512], P(('cfg', 'expert')), parts along dimension 0, may hold values from 0 to 16383, as said below
- gates: float32 [128, 512], P(('cfg', 'expert')), parts along dimension 0, may hold values from 0.1 to 1
- capacity: int32 [2], P('cfg'), parts along dimension 0, may hold values from 256 to 512
- w_gate: bfloat16 [64, 2048, 1024], P('expert', None, 'ffn'), may hold values from -0.125 to 0.125
- w_up: bfloat16 [64, 2048, 1024], P('expert', None, 'ffn'), may hold values from -0.125 to 0.125
- w_down: bfloat16 [64, 1024, 2048], P('expert', 'ffn'), may hold values from -0.1875 to 0.1875
Outputs:
- mixed: bfloat16 [32768, 2048], P(('cfg', 'expert'), 'ffn'), parts along dimension 0
There are 2 independent parts, one for each index of `cfg`. A program takes and returns all parts, laid end to end along the dimension named above; an argument that names none is the same for every part. Nothing has to cross between parts.
Inputs may be any that keep to these rules, and one draw needn't show every extreme that they name: `chosen`: each row lists 512 different tokens; at most 16 of one row's tokens lie in one aligned block of 256 tokens, and every row has exactly 16 in some block.
All inputs are finite; a program needn't handle non-finite values.
Results may differ from a plain program's by a relative error of at most 0.013.
Values may be sent and summed in bfloat16 or wider, within the bound.
No kernel may reach another device: no remote copies, remote signals or barrier semaphores. Data moves between devices by JAX's collectives and lax.ppermute only.
A program may use at most 64 MiB of HBM per device.

v0:
```python
import jax
import jax.numpy as jnp
from jax import lax
from jax.sharding import Mesh
from jax.sharding import PartitionSpec as P


EXPERT = ("expert_0", "expert_1")
CFG_EXPERT = ("cfg", "expert_0", "expert_1")


def hop(array, step):
    peers = lax.axis_size("ffn")
    return lax.ppermute(array, "ffn", [(k, (k + step) % peers) for k in range(peers)])


def one_hot(rows, columns):
    return (rows[:, None] == columns[None, :]).astype(jnp.bfloat16)


def mm(a, b):
    return jnp.dot(a, b, preferred_element_type=jnp.float32)


def swap(tiles):
    return lax.all_to_all(tiles, EXPERT, split_axis=0, concat_axis=0, tiled=True)


def shards(tokens, chosen, gates, capacity, w_gate, w_up, w_down):
    experts_n = lax.axis_size(EXPERT)
    ffn_n = lax.axis_size("ffn")
    me = lax.axis_index("ffn")
    tok_dev, width = tokens.shape
    picked_ids = chosen[0]
    listed = picked_ids.shape[0]
    slot_depth = 2 * listed // experts_n
    depth = slot_depth // ffn_n
    held = experts_n * depth

    positions = jnp.arange(listed, dtype=jnp.int32)
    alive = positions < capacity[0]
    weights = jnp.where(alive, gates[0], jnp.zeros_like(gates[0]))
    source = picked_ids // tok_dev
    offset = picked_ids - source * tok_dev
    member = one_hot(source, jnp.arange(experts_n, dtype=jnp.int32))
    earlier = (positions[:, None] > positions[None, :]).astype(jnp.bfloat16)
    before = mm(earlier, member)
    rank_in = jnp.sum(before * member.astype(jnp.float32), axis=1).astype(jnp.int32)
    place_in = (rank_in % ffn_n) * depth + rank_in // ffn_n
    asked = jnp.where(alive, offset + 1, 0).astype(jnp.bfloat16)
    spread = one_hot(place_in, jnp.arange(slot_depth, dtype=jnp.int32)) * asked[:, None]
    request = lax.dot_general(
        member, spread, (((0,), (0,)), ((), ())), preferred_element_type=jnp.float32
    )
    request = request.astype(jnp.int32) - 1
    requested = swap(request.reshape(experts_n, 1, slot_depth))
    requested = requested.reshape(experts_n, ffn_n, depth)

    pieces = jnp.stack([tokens, hop(tokens, 1), hop(tokens, 2), hop(tokens, -1)])

    mine = lax.dynamic_index_in_dim(requested, me, 1, keepdims=False).reshape(-1)
    selects = one_hot(mine, jnp.arange(tok_dev, dtype=jnp.int32))
    rows = jnp.concatenate(
        [
            mm(
                selects,
                lax.dynamic_index_in_dim(pieces, lax.rem(me + ffn_n - b, ffn_n), 0, keepdims=False),
            ).astype(jnp.bfloat16)
            for b in range(ffn_n)
        ],
        axis=1,
    )
    rows, shared = lax.optimization_barrier((rows, (w_gate[0], w_up[0], w_down[0])))
    arrived = swap(rows.reshape(experts_n, depth, -1)).reshape(held, -1)

    own_gate, _, _ = shared
    half = own_gate.shape[1] // 2
    left = [hop(w, 1) for w in shared]
    right = [hop(w, -1) for w in shared]
    far_left = [hop(left[0][:, :half], 1), hop(left[1][:, :half], 1), hop(left[2][:half], 1)]
    far_right = [hop(right[0][:, half:], -1), hop(right[1][:, half:], -1), hop(right[2][half:], -1)]

    slot_of = source * depth + rank_in // ffn_n
    at_mine = (rank_in % ffn_n) == me
    gate_of = jnp.sum(
        jnp.where(
            (jnp.arange(held, dtype=jnp.int32)[:, None] == slot_of[None, :])
            & at_mine[None, :],
            weights[None, :],
            0.0,
        ),
        axis=1,
    )

    summed = 0.0
    for gate_cols, up_cols, down_rows in (shared, left, right, far_left, far_right):
        gate_part = mm(arrived, gate_cols)
        up_part = mm(arrived, up_cols)
        hidden = (jax.nn.silu(gate_part) * up_part).astype(jnp.bfloat16)
        summed = summed + mm(hidden, down_rows)
    contribution = (gate_of[:, None] * summed).astype(jnp.bfloat16)
    returned = swap(contribution.reshape(experts_n, depth, -1))

    tiles = jnp.moveaxis(returned.reshape(held, ffn_n, width), 1, 0)
    tiles = lax.all_to_all(tiles, "ffn", split_axis=0, concat_axis=0, tiled=True)
    slot_token = jnp.moveaxis(requested, 1, 0).reshape(-1)
    placement = one_hot(jnp.arange(tok_dev, dtype=jnp.int32), slot_token)
    return mm(placement, tiles.reshape(ffn_n * held, width)).astype(jnp.bfloat16)


def solution(mesh):
    split = Mesh(
        mesh.devices.reshape(
            mesh.shape["cfg"], mesh.shape["expert"] // 2, 2, mesh.shape["ffn"]
        ),
        ("cfg", "expert_0", "expert_1", "ffn"),
    )
    return jax.shard_map(
        shards,
        mesh=split,
        in_specs=(
            P(CFG_EXPERT, "ffn"),
            P(CFG_EXPERT, None),
            P(CFG_EXPERT, None),
            P("cfg"),
            P(EXPERT, None, "ffn"),
            P(EXPERT, None, "ffn"),
            P(EXPERT, "ffn", None),
        ),
        out_specs=P(CFG_EXPERT, "ffn"),
        check_vma=False,
    )
```

profile of v0, /device:TPU:33, one launch (start us, length us, event | category | flops | bytes accessed | tf_op | source)
XLA Modules:
  0.0 374.0 jit_solution(16900583589007559632)
XLA Ops:
  0.0 5.8 %collective-permute-start.1 = (bf16[256,512]{1,0:T(8,128)(2,1)}, bf16[256,512]{1,0:T(8,128)(2,1)S(1)}, u32[]{:S(2)}, u32[]{:S(2)}) collective-permute-start(bf16[256,512]{1,0:T(8,128)(2,1)} %param.7), channel_id=1, source_target_pairs={{0,2},{1,3},{2,0},{3,1},{4,6},{5,7},{6,4},{7,5},{8,10},{9,11},{10,... | collective-permute-start | bytes 786440 | tf_op jit(solution)/shard_map/ppermute | solution.py:14
  5.8 2.7 collective-permute-start.2
  8.4 2.7 collective-permute-start
  13.9 47.5 %all-to-all-start = ((s32[64,1,16]{2,1,0:T(1,128)}), s32[64,1,16]{2,1,0:T(1,128)S(1)}, u32[]{:S(2)}, u32[]{:S(2)}) async-start(s32[64,1,16]{2,1,0:T(1,128)} %copy.22), calls=%async_computation | async-start | bytes 65536 | tf_op jit(solution)/shard_map/all_to_all | solution.py:26
  61.4 21.8 %all-to-all-done = s32[64,1,16]{2,1,0:T(1,128)S(1)} async-done(((s32[64,1,16]{2,1,0:T(1,128)}), s32[64,1,16]{2,1,0:T(1,128)S(1)}, u32[]{:S(2)}, u32[]{:S(2)}) %all-to-all-start) | async-done | bytes 4128 | tf_op jit(solution)/shard_map/all_to_all | solution.py:26
  87.0 6.3 %all-to-all-start.1 = ((bf16[64,4,2048]{2,1,0:T(4,128)(2,1)}), bf16[64,4,2048]{2,1,0:T(4,128)(2,1)S(1)}, u32[]{:S(2)}, u32[]{:S(2)}) async-start(bf16[64,4,2048]{2,1,0:T(4,128)(2,1)} %reshape.181), calls=%async_computation.1 | async-start | bytes 2097152 | tf_op jit(solution)/shard_map/all_to_all | solution.py:26
  93.3 2.4 collective-permute-start.3
  95.7 2.0 collective-permute-start.4
  97.7 4.3 %collective-permute-start.5 = (bf16[256,2048]{1,0:T(8,128)(2,1)}, bf16[256,2048]{1,0:T(8,128)(2,1)S(1)}, u32[]{:S(2)}, u32[]{:S(2)}) collective-permute-start(bf16[256,2048]{1,0:T(8,128)(2,1)} %bitcast.66), channel_id=1, source_target_pairs={{0,1},{1,2},{2,3},{3,0},{4,5},{5,6},{6,7},{7,4},{8,9},{9,10},{10,1... | collective-permute-start | bytes 3145736 | tf_op jit(solution)/shard_map/ppermute | solution.py:14
  102.0 2.3 collective-permute-start.6
  104.3 3.4 collective-permute-start.7
  107.7 12.1 %collective-permute-done.3 = bf16[2048,256]{1,0:T(8,128)(2,1)S(1)} collective-permute-done((bf16[2048,256]{1,0:T(8,128)(2,1)}, bf16[2048,256]{1,0:T(8,128)(2,1)S(1)}, u32[]{:S(2)}, u32[]{:S(2)}) %collective-permute-start.3) | collective-permute-done | bytes 1048608 | tf_op jit(solution)/shard_map/ppermute | solution.py:14
  119.8 2.7 collective-permute-start.8
  123.4 18.8 %collective-permute-done.4 = bf16[2048,256]{1,0:T(8,128)(2,1)S(1)} collective-permute-done((bf16[2048,256]{1,0:T(8,128)(2,1)}, bf16[2048,256]{1,0:T(8,128)(2,1)S(1)}, u32[]{:S(2)}, u32[]{:S(2)}) %collective-permute-start.4) | collective-permute-done | bytes 1048608 | tf_op jit(solution)/shard_map/ppermute | solution.py:14
  142.2 1.9 collective-permute-start.9
  145.2 19.5 %collective-permute-done.5 = bf16[256,2048]{1,0:T(8,128)(2,1)S(1)} collective-permute-done((bf16[256,2048]{1,0:T(8,128)(2,1)}, bf16[256,2048]{1,0:T(8,128)(2,1)S(1)}, u32[]{:S(2)}, u32[]{:S(2)}) %collective-permute-start.5) | collective-permute-done | bytes 1048608 | tf_op jit(solution)/shard_map/ppermute | solution.py:14
  164.7 1.9 collective-permute-start.10
  167.5 1.9 collective-permute-start.11
  170.3 4.6 %collective-permute-start.12 = (bf16[2048,128]{1,0:T(8,128)(2,1)}, bf16[2048,128]{1,0:T(8,128)(2,1)}, u32[]{:S(2)}, u32[]{:S(2)}) collective-permute-start(bf16[2048,128]{1,0:T(8,128)(2,1)} %slice.27), channel_id=1, source_target_pairs={{0,3},{1,0},{2,1},{3,2},{4,7},{5,4},{6,5},{7,6},{8,11},{9,8},{10,9... | collective-permute-start | bytes 1572872 | tf_op jit(solution)/shard_map/ppermute | solution.py:14
  175.8 3.4 collective-permute-start.13
  180.0 21.8 %all-to-all-done.1 = bf16[64,4,2048]{2,1,0:T(4,128)(2,1)S(1)} async-done(((bf16[64,4,2048]{2,1,0:T(4,128)(2,1)}), bf16[64,4,2048]{2,1,0:T(4,128)(2,1)S(1)}, u32[]{:S(2)}, u32[]{:S(2)}) %all-to-all-start.1) | async-done | bytes 1048608 | tf_op jit(solution)/shard_map/all_to_all | solution.py:26
  202.1 2.4 fusion.67
  204.5 4.0 %collective-permute-start.14 = (bf16[128,2048]{1,0:T(8,128)(2,1)}, bf16[128,2048]{1,0:T(8,128)(2,1)}, u32[]{:S(2)}, u32[]{:S(2)}) collective-permute-start(bf16[128,2048]{1,0:T(8,128)(2,1)} %slice.29), channel_id=1, source_target_pairs={{0,3},{1,0},{2,1},{3,2},{4,7},{5,4},{6,5},{7,6},{8,11},{9,8},{10,9... | collective-permute-start | bytes 1572872 | tf_op jit(solution)/shard_map/ppermute | solution.py:14
  211.1 2.0 fusion.35
  213.1 1.7 fusion.69
  214.8 4.2 %fusion.5 = f32[256,2048]{1,0:T(8,128)} fusion(bf16[256,2048]{1,0:T(8,128)(2,1)} %bitcast.68, bf16[256,2048]{1,0:T(8,128)(2,1)S(1)} %reshape.182, bf16[2048,256]{1,0:T(8,128)(2,1)} %bitcast.71, f32[256,256]{1,0:T(8,128)} %fusion.67), kind=kOutput, calls=%fused_computation.13 | convolution fusion | flops 537264128 | bytes 5505024 | tf_op jit(solution)/shard_map/dot_general | solution.py:22
  220.5 4.9 %convolution_add_fusion.1 = f32[256,2048]{1,0:T(8,128)} fusion(f32[256,2048]{1,0:T(8,128)} %fusion.5, bf16[256,2048]{1,0:T(8,128)(2,1)} %copy-done.4, f32[256,256]{1,0:T(8,128)} %fusion.68, bf16[256,2048]{1,0:T(8,128)(2,1)S(1)} %reshape.182, bf16[2048,256]{1,0:T(8,128)(2,1)} %copy-done.2), kind=kOutput, calls=%fused_computation.4 | convolution fusion | flops 537788416 | bytes 7602176 | tf_op jit(solution)/shard_map/dot_general | solution.py:22
  225.4 3.3 fusion.36
  228.7 5.1 %fusion.3 = bf16[256,2048]{1,0:T(8,128)(2,1)} fusion(f32[256,2048]{1,0:T(8,128)} %fusion.36, f32[256,2048]{1,0:T(8,128)S(1)} %fusion.35, f32[256,2048]{1,0:T(8,128)} %convolution_add_fusion.1, bf16[256,2048]{1,0:T(8,128)(2,1)} %copy-done.3, f32[256]{0:T(256)S(1)} %select_reduce_fusion, f32[256,256]{1,0:T(8,128)S(1)} %fusion.69, ...), kind=kOutput, calls=%fused_computation.5 | convolution fusion | flops 539885568 | bytes 10748928 | tf_op jit(solution)/shard_map/dot_general | solution.py:22
  235.3 120.3 %all_to_all.20 = bf16[64,4,2048]{2,1,0:T(4,128)(2,1)S(1)} all-to-all(bf16[64,4,2048]{2,1,0:T(4,128)(2,1)S(1)} %reshape.183), channel_id=1, replica_groups=mesh['cfg'=2,'expert_0'=32,'expert_1'=2,'ffn'=4] {'expert_0','expert_1'}, dimensions={0} | all-to-all | bytes 2097152 | tf_op jit(solution)/shard_map/all_to_all | solution.py:26
  357.5 3.6 all-to-all-start.3
  361.3 11.5 %all-to-all-done.3 = bf16[4,256,512]{2,1,0:T(8,128)(2,1)S(1)} async-done(((bf16[4,256,512]{2,1,0:T(8,128)(2,1)}), bf16[4,256,512]{2,1,0:T(8,128)(2,1)S(1)}, u32[]{:S(2)}, u32[]{:S(2)}) %all-to-all-start.3) | async-done | bytes 1048608 | tf_op jit(solution)/shard_map/all_to_all | solution.py:105
  (63 shorter events, 20.3 us)
Async XLA Ops:
  0.0 83.5 %collective-permute-start.1 = (bf16[256,512]{1,0:T(8,128)(2,1)}, bf16[256,512]{1,0:T(8,128)(2,1)S(1)}, u32[]{:S(2)}, u32[]{:S(2)}) collective-permute-start(bf16[256,512]{1,0:T(8,128)(2,1)} %param.7), channel_id=1, source_target_pairs={{0,2},{1,3},{2,0},{3,1},{4,6},{5,7},{6,4},{7,5},{8,10},{9,11},{10,... | collective-permute-start | bytes 786440 | tf_op jit(solution)/shard_map/ppermute | solution.py:14
  5.8 77.7 %collective-permute-start.2 = (bf16[256,512]{1,0:T(8,128)(2,1)}, bf16[256,512]{1,0:T(8,128)(2,1)S(1)}, u32[]{:S(2)}, u32[]{:S(2)}) collective-permute-start(bf16[256,512]{1,0:T(8,128)(2,1)} %param.7), channel_id=1, source_target_pairs={{0,3},{1,0},{2,1},{3,2},{4,7},{5,4},{6,5},{7,6},{8,11},{9,8},{10,9... | collective-permute-start | bytes 786440 | tf_op jit(solution)/shard_map/ppermute | solution.py:14
  8.4 75.0 %collective-permute-start = (bf16[256,512]{1,0:T(8,128)(2,1)}, bf16[256,512]{1,0:T(8,128)(2,1)S(1)}, u32[]{:S(2)}, u32[]{:S(2)}) collective-permute-start(bf16[256,512]{1,0:T(8,128)(2,1)} %param.7), channel_id=1, source_target_pairs={{0,1},{1,2},{2,3},{3,0},{4,5},{5,6},{6,7},{7,4},{8,9},{9,10},{10,1... | collective-permute-start | bytes 786440 | tf_op jit(solution)/shard_map/ppermute | solution.py:14
  13.9 69.3 %all-to-all-start = ((s32[64,1,16]{2,1,0:T(1,128)}), s32[64,1,16]{2,1,0:T(1,128)S(1)}, u32[]{:S(2)}, u32[]{:S(2)}) async-start(s32[64,1,16]{2,1,0:T(1,128)} %copy.22), calls=%async_computation | async-start | bytes 65536 | tf_op jit(solution)/shard_map/all_to_all | solution.py:26
  85.8 36.6 %copy-start.6 = (f32[1,512]{1,0:T(1,128)S(1)}, f32[1,512]{1,0:T(1,128)}, u32[]{:S(2)}) copy-start(f32[1,512]{1,0:T(1,128)} %param.9) | copy-start | bytes 6148
  85.8 36.6 %copy-start.5 = (s32[1,512]{1,0:T(1,128)S(1)}, s32[1,512]{1,0:T(1,128)}, u32[]{:S(2)}) copy-start(s32[1,512]{1,0:T(1,128)} %param.8) | copy-start | bytes 6148
  87.0 114.8 %all-to-all-start.1 = ((bf16[64,4,2048]{2,1,0:T(4,128)(2,1)}), bf16[64,4,2048]{2,1,0:T(4,128)(2,1)S(1)}, u32[]{:S(2)}, u32[]{:S(2)}) async-start(bf16[64,4,2048]{2,1,0:T(4,128)(2,1)} %reshape.181), calls=%async_computation.1 | async-start | bytes 2097152 | tf_op jit(solution)/shard_map/all_to_all | solution.py:26
  93.3 26.4 %collective-permute-start.3 = (bf16[2048,256]{1,0:T(8,128)(2,1)}, bf16[2048,256]{1,0:T(8,128)(2,1)S(1)}, u32[]{:S(2)}, u32[]{:S(2)}) collective-permute-start(bf16[2048,256]{1,0:T(8,128)(2,1)} %bitcast.62), channel_id=1, source_target_pairs={{0,1},{1,2},{2,3},{3,0},{4,5},{5,6},{6,7},{7,4},{8,9},{9,10},{10,1... | collective-permute-start | bytes 3145736 | tf_op jit(solution)/shard_map/ppermute | solution.py:14
  95.7 46.5 %collective-permute-start.4 = (bf16[2048,256]{1,0:T(8,128)(2,1)}, bf16[2048,256]{1,0:T(8,128)(2,1)S(1)}, u32[]{:S(2)}, u32[]{:S(2)}) collective-permute-start(bf16[2048,256]{1,0:T(8,128)(2,1)} %bitcast.69), channel_id=1, source_target_pairs={{0,1},{1,2},{2,3},{3,0},{4,5},{5,6},{6,7},{7,4},{8,9},{9,10},{10,1... | collective-permute-start | bytes 3145736 | tf_op jit(solution)/shard_map/ppermute | solution.py:14
  97.7 67.0 %collective-permute-start.5 = (bf16[256,2048]{1,0:T(8,128)(2,1)}, bf16[256,2048]{1,0:T(8,128)(2,1)S(1)}, u32[]{:S(2)}, u32[]{:S(2)}) collective-permute-start(bf16[256,2048]{1,0:T(8,128)(2,1)} %bitcast.66), channel_id=1, source_target_pairs={{0,1},{1,2},{2,3},{3,0},{4,5},{5,6},{6,7},{7,4},{8,9},{9,10},{10,1... | collective-permute-start | bytes 3145736 | tf_op jit(solution)/shard_map/ppermute | solution.py:14
  102.0 65.5 %collective-permute-start.6 = (bf16[2048,256]{1,0:T(8,128)(2,1)}, bf16[2048,256]{1,0:T(8,128)(2,1)S(1)}, u32[]{:S(2)}, u32[]{:S(2)}) collective-permute-start(bf16[2048,256]{1,0:T(8,128)(2,1)} %bitcast.63), channel_id=1, source_target_pairs={{0,3},{1,0},{2,1},{3,2},{4,7},{5,4},{6,5},{7,6},{8,11},{9,8},{10,9... | collective-permute-start | bytes 3145736 | tf_op jit(solution)/shard_map/ppermute | solution.py:14
  104.3 66.0 %collective-permute-start.7 = (bf16[2048,256]{1,0:T(8,128)(2,1)}, bf16[2048,256]{1,0:T(8,128)(2,1)S(1)}, u32[]{:S(2)}, u32[]{:S(2)}) collective-permute-start(bf16[2048,256]{1,0:T(8,128)(2,1)} %bitcast.70), channel_id=1, source_target_pairs={{0,3},{1,0},{2,1},{3,2},{4,7},{5,4},{6,5},{7,6},{8,11},{9,8},{10,9... | collective-permute-start | bytes 3145736 | tf_op jit(solution)/shard_map/ppermute | solution.py:14
  119.8 56.0 %collective-permute-start.8 = (bf16[256,2048]{1,0:T(8,128)(2,1)}, bf16[256,2048]{1,0:T(8,128)(2,1)S(1)}, u32[]{:S(2)}, u32[]{:S(2)}) collective-permute-start(bf16[256,2048]{1,0:T(8,128)(2,1)} %bitcast.67), channel_id=1, source_target_pairs={{0,3},{1,0},{2,1},{3,2},{4,7},{5,4},{6,5},{7,6},{8,11},{9,8},{10,9... | collective-permute-start | bytes 3145736 | tf_op jit(solution)/shard_map/ppermute | solution.py:14
  142.2 33.5 %copy-start.2 = (bf16[2048,256]{1,0:T(8,128)(2,1)}, bf16[2048,256]{1,0:T(8,128)(2,1)S(1)}, u32[]{:S(2)}) copy-start(bf16[2048,256]{1,0:T(8,128)(2,1)S(1)} %collective-permute-done.4) | copy-start | bytes 3145732
  142.2 62.3 %collective-permute-start.9 = (bf16[2048,128]{1,0:T(8,128)(2,1)}, bf16[2048,128]{1,0:T(8,128)(2,1)}, u32[]{:S(2)}, u32[]{:S(2)}) collective-permute-start(bf16[2048,128]{1,0:T(8,128)(2,1)} %slice.24), channel_id=1, source_target_pairs={{0,1},{1,2},{2,3},{3,0},{4,5},{5,6},{6,7},{7,4},{8,9},{9,10},{10,1... | collective-permute-start | bytes 1572872 | tf_op jit(solution)/shard_map/ppermute | solution.py:14
  164.7 14.5 %copy-start.4 = (bf16[256,2048]{1,0:T(8,128)(2,1)}, bf16[256,2048]{1,0:T(8,128)(2,1)S(1)}, u32[]{:S(2)}) copy-start(bf16[256,2048]{1,0:T(8,128)(2,1)S(1)} %collective-permute-done.5) | copy-start | bytes 3145732
  164.7 46.4 %collective-permute-start.10 = (bf16[2048,128]{1,0:T(8,128)(2,1)}, bf16[2048,128]{1,0:T(8,128)(2,1)}, u32[]{:S(2)}, u32[]{:S(2)}) collective-permute-start(bf16[2048,128]{1,0:T(8,128)(2,1)} %slice.25), channel_id=1, source_target_pairs={{0,1},{1,2},{2,3},{3,0},{4,5},{5,6},{6,7},{7,4},{8,9},{9,10},{10,1... | collective-permute-start | bytes 1572872 | tf_op jit(solution)/shard_map/ppermute | solution.py:14
  167.5 11.7 %copy-start = (bf16[2048,256]{1,0:T(8,128)(2,1)}, bf16[2048,256]{1,0:T(8,128)(2,1)S(1)}, u32[]{:S(2)}) copy-start(bf16[2048,256]{1,0:T(8,128)(2,1)S(1)} %collective-permute-done.6) | copy-start | bytes 3145732
  167.5 43.7 %collective-permute-start.11 = (bf16[128,2048]{1,0:T(8,128)(2,1)}, bf16[128,2048]{1,0:T(8,128)(2,1)}, u32[]{:S(2)}, u32[]{:S(2)}) collective-permute-start(bf16[128,2048]{1,0:T(8,128)(2,1)} %slice.26), channel_id=1, source_target_pairs={{0,1},{1,2},{2,3},{3,0},{4,5},{5,6},{6,7},{7,4},{8,9},{9,10},{10,1... | collective-permute-start | bytes 1572872 | tf_op jit(solution)/shard_map/ppermute | solution.py:14
  170.3 8.9 %copy-start.1 = (bf16[2048,256]{1,0:T(8,128)(2,1)}, bf16[2048,256]{1,0:T(8,128)(2,1)S(1)}, u32[]{:S(2)}) copy-start(bf16[2048,256]{1,0:T(8,128)(2,1)S(1)} %collective-permute-done.7) | copy-start | bytes 3145732
  170.3 48.7 %collective-permute-start.12 = (bf16[2048,128]{1,0:T(8,128)(2,1)}, bf16[2048,128]{1,0:T(8,128)(2,1)}, u32[]{:S(2)}, u32[]{:S(2)}) collective-permute-start(bf16[2048,128]{1,0:T(8,128)(2,1)} %slice.27), channel_id=1, source_target_pairs={{0,3},{1,0},{2,1},{3,2},{4,7},{5,4},{6,5},{7,6},{8,11},{9,8},{10,9... | collective-permute-start | bytes 1572872 | tf_op jit(solution)/shard_map/ppermute | solution.py:14
  175.8 3.4 copy-start.3
  175.8 49.6 %collective-permute-start.13 = (bf16[2048,128]{1,0:T(8,128)(2,1)}, bf16[2048,128]{1,0:T(8,128)(2,1)}, u32[]{:S(2)}, u32[]{:S(2)}) collective-permute-start(bf16[2048,128]{1,0:T(8,128)(2,1)} %slice.28), channel_id=1, source_target_pairs={{0,3},{1,0},{2,1},{3,2},{4,7},{5,4},{6,5},{7,6},{8,11},{9,8},{10,9... | collective-permute-start | bytes 1572872 | tf_op jit(solution)/shard_map/ppermute | solution.py:14
  204.5 20.9 %collective-permute-start.14 = (bf16[128,2048]{1,0:T(8,128)(2,1)}, bf16[128,2048]{1,0:T(8,128)(2,1)}, u32[]{:S(2)}, u32[]{:S(2)}) collective-permute-start(bf16[128,2048]{1,0:T(8,128)(2,1)} %slice.29), channel_id=1, source_target_pairs={{0,3},{1,0},{2,1},{3,2},{4,7},{5,4},{6,5},{7,6},{8,11},{9,8},{10,9... | collective-permute-start | bytes 1572872 | tf_op jit(solution)/shard_map/ppermute | solution.py:14
  357.5 15.3 %all-to-all-start.3 = ((bf16[4,256,512]{2,1,0:T(8,128)(2,1)}), bf16[4,256,512]{2,1,0:T(8,128)(2,1)S(1)}, u32[]{:S(2)}, u32[]{:S(2)}) async-start(bf16[4,256,512]{2,1,0:T(8,128)(2,1)} %copy.26), calls=%async_computation.3 | async-start | bytes 2097152 | tf_op jit(solution)/shard_map/all_to_all | solution.py:105
where the time goes:
time: 378 us; the launch traced here: 374 us
  blocking collectives  120 us (32%)
  waiting for transfers between devices  106 us (28%)
  starting transfers between devices  103 us (27%)
  matrix products  30.5 us (8%)
  local copies, waits for them, and re-layouts  11.1 us (3%)
    all_to_all x1, blocking collectives, swap(): lax.all_to_all(tiles, EXPERT, split_axis=0, concat_axis=0, tiled=True)  120 us
    all_to_all x2, starting transfers between devices, swap(): lax.all_to_all(tiles, EXPERT, split_axis=0, concat_axis=0, tiled=True)  53.7 us
    ppermute x15, waiting for transfers between devices, hop(): lax.ppermute(array, 'ffn', [(k, (k + step) % peers) for k in range(peers)])  50.4 us
    ppermute x15, starting transfers between devices, hop(): lax.ppermute(array, 'ffn', [(k, (k + step) % peers) for k in range(peers)])  45.9 us
    all_to_all x2, waiting for transfers between devices, swap(): lax.all_to_all(tiles, EXPERT, split_axis=0, concat_axis=0, tiled=True)  43.6 us
    dot_general x16, matrix products, mm(): return jnp.dot(a, b, preferred_element_type=jnp.float32)  30.2 us
    all_to_all x1, waiting for transfers between devices, shards(): lax.all_to_all(tiles, 'ffn', split_axis=0, concat_axis=0, tiled=True)  11.5 us
  transfers between devices with their start and end apart: 18, of which 6 were waited for; matrix products, arithmetic and copies ran while one was open for 7% of the time, Pallas kernels for 0%

commit v1 on v0

--- a/solution.py
+++ b/solution.py
@@ -92,12 +92,13 @@
         axis=1,
     )
 
-    summed = 0.0
-    for gate_cols, up_cols, down_rows in (shared, left, right, far_left, far_right):
-        gate_part = mm(arrived, gate_cols)
-        up_part = mm(arrived, up_cols)
-        hidden = (jax.nn.silu(gate_part) * up_part).astype(jnp.bfloat16)
-        summed = summed + mm(hidden, down_rows)
+    joined = []
+    for k, dim in ((0, 1), (1, 1), (2, 0)):
+        parts = [g[k] for g in (shared, left, right, far_left, far_right)]
+        joined.append(jnp.concatenate(parts, axis=dim))
+    gate_cols, up_cols, down_rows = lax.optimization_barrier(tuple(joined))
+    hidden = (jax.nn.silu(mm(arrived, gate_cols)) * mm(arrived, up_cols)).astype(jnp.bfloat16)
+    summed = mm(hidden, down_rows)
     contribution = (gate_of[:, None] * summed).astype(jnp.bfloat16)
     returned = swap(contribution.reshape(experts_n, depth, -1))
 

time: 378 us -> 366 us (0.968)
  matrix products: 30.5 us -> 12.3 us
  blocking collectives: 120 us -> 133 us
  waiting for transfers between devices: 106 us -> 99.2 us
    all_to_all x2, waiting for transfers between devices: 43.6 us -> 22.4 us  [swap(): lax.all_to_all(tiles, EXPERT, split_axis=0, concat_axis=0, tiled=True)]
    dot_general x16 -> x8, matrix products: 30.2 us -> 11.9 us  [mm(): return jnp.dot(a, b, preferred_element_type=jnp.float32)]
    ppermute x15, waiting for transfers between devices: 50.4 us -> 65.5 us  [hop(): lax.ppermute(array, 'ffn', [(k, (k + step) % peers) for k in range(peers)])]
    all_to_all x1, blocking collectives: 120 us -> 133 us  [swap(): lax.all_to_all(tiles, EXPERT, split_axis=0, concat_axis=0, tiled=True)]
    unnamed x14 -> x23, local copies, waits for them, and re-layouts: 0.03 us -> 6.51 us
  transfers between devices with their start and end apart: 18 -> 18, of which waited for: 6 -> 11; matrix products, arithmetic and copies ran while one was open for 7% -> 3% of each run, Pallas kernels for 0% -> 0%
where the time goes in v1:
time: 366 us; the launch traced here: 362 us
  blocking collectives  133 us (36%)
  starting transfers between devices  102 us (28%)
  waiting for transfers between devices  99.2 us (27%)
  local copies, waits for them, and re-layouts  13 us (4%)
  matrix products  12.3 us (3%)
    all_to_all x1, blocking collectives, swap(): lax.all_to_all(tiles, EXPERT, split_axis=0, concat_axis=0, tiled=True)  133 us
    ppermute x15, waiting for transfers between devices, hop(): lax.ppermute(array, 'ffn', [(k, (k + step) % peers) for k in range(peers)])  65.5 us
    all_to_all x2, starting transfers between devices, swap(): lax.all_to_all(tiles, EXPERT, split_axis=0, concat_axis=0, tiled=True)  53.7 us
    ppermute x15, starting transfers between devices, hop(): lax.ppermute(array, 'ffn', [(k, (k + step) % peers) for k in range(peers)])  44.4 us
    all_to_all x2, waiting for transfers between devices, swap(): lax.all_to_all(tiles, EXPERT, split_axis=0, concat_axis=0, tiled=True)  22.4 us
    dot_general x8, matrix products, mm(): return jnp.dot(a, b, preferred_element_type=jnp.float32)  11.9 us
    all_to_all x1, waiting for transfers between devices, shards(): lax.all_to_all(tiles, 'ffn', split_axis=0, concat_axis=0, tiled=True)  11.2 us
  transfers between devices with their start and end apart: 18, of which 11 were waited for; matrix products, arithmetic and copies ran while one was open for 3% of the time, Pallas kernels for 0%

profile of v1, /device:TPU:33, one launch (start us, length us, event | category | flops | bytes accessed | tf_op | source)
XLA Modules:
  0.0 362.1 jit_solution(10681064075067883523)
XLA Ops:
  0.0 5.6 %collective-permute-start.2 = (bf16[256,512]{1,0:T(8,128)(2,1)}, bf16[256,512]{1,0:T(8,128)(2,1)S(1)}, u32[]{:S(2)}, u32[]{:S(2)}) collective-permute-start(bf16[256,512]{1,0:T(8,128)(2,1)} %param.7), channel_id=1, source_target_pairs={{0,3},{1,0},{2,1},{3,2},{4,7},{5,4},{6,5},{7,6},{8,11},{9,8},{10,9... | collective-permute-start | bytes 786440 | tf_op jit(solution)/shard_map/ppermute | solution.py:14
  5.6 2.2 collective-permute-start.1
  7.8 2.7 collective-permute-start
  13.3 47.5 %all-to-all-start = ((s32[64,1,16]{2,1,0:T(1,128)}), s32[64,1,16]{2,1,0:T(1,128)S(1)}, u32[]{:S(2)}, u32[]{:S(2)}) async-start(s32[64,1,16]{2,1,0:T(1,128)} %copy.22), calls=%async_computation | async-start | bytes 65536 | tf_op jit(solution)/shard_map/all_to_all | solution.py:26
  60.8 21.8 %all-to-all-done = s32[64,1,16]{2,1,0:T(1,128)S(1)} async-done(((s32[64,1,16]{2,1,0:T(1,128)}), s32[64,1,16]{2,1,0:T(1,128)S(1)}, u32[]{:S(2)}, u32[]{:S(2)}) %all-to-all-start) | async-done | bytes 4128 | tf_op jit(solution)/shard_map/all_to_all | solution.py:26
  86.5 6.3 %all-to-all-start.1 = ((bf16[64,4,2048]{2,1,0:T(4,128)(2,1)}), bf16[64,4,2048]{2,1,0:T(4,128)(2,1)S(1)}, u32[]{:S(2)}, u32[]{:S(2)}) async-start(bf16[64,4,2048]{2,1,0:T(4,128)(2,1)} %reshape.181), calls=%async_computation.1 | async-start | bytes 2097152 | tf_op jit(solution)/shard_map/all_to_all | solution.py:26
  92.9 3.6 collective-permute-start.3
  96.5 3.0 collective-permute-start.4
  99.5 2.4 collective-permute-start.7
  102.1 4.2 %collective-permute-start.8 = (bf16[2048,256]{1,0:T(8,128)(2,1)}, bf16[2048,256]{1,0:T(8,128)(2,1)S(1)}, u32[]{:S(2)}, u32[]{:S(2)}) collective-permute-start(bf16[2048,256]{1,0:T(8,128)(2,1)} %bitcast.50), channel_id=1, source_target_pairs={{0,3},{1,0},{2,1},{3,2},{4,7},{5,4},{6,5},{7,6},{8,11},{9,8},{10,9... | collective-permute-start | bytes 3145736 | tf_op jit(solution)/shard_map/ppermute | solution.py:14
  106.3 1.5 constant_dynamic-update-slice_fusion.4
  107.8 2.0 collective-permute-start.11
  110.9 8.2 %collective-permute-done.3 = bf16[2048,256]{1,0:T(8,128)(2,1)S(1)} collective-permute-done((bf16[2048,256]{1,0:T(8,128)(2,1)S(1)}, bf16[2048,256]{1,0:T(8,128)(2,1)S(1)}, u32[]{:S(2)}, u32[]{:S(2)}) %collective-permute-start.3) | collective-permute-done | bytes 1048608 | tf_op jit(solution)/shard_map/ppermute | solution.py:14
  119.1 2.7 collective-permute-start.12
  121.9 2.7 collective-permute-start.5
  124.7 16.9 %collective-permute-done.7 = bf16[2048,256]{1,0:T(8,128)(2,1)S(1)} collective-permute-done((bf16[2048,256]{1,0:T(8,128)(2,1)}, bf16[2048,256]{1,0:T(8,128)(2,1)S(1)}, u32[]{:S(2)}, u32[]{:S(2)}) %collective-permute-start.7) | collective-permute-done | bytes 1048608 | tf_op jit(solution)/shard_map/ppermute | solution.py:14
  141.6 2.7 collective-permute-start.6
  144.6 2.7 collective-permute-start.9
  147.4 16.6 %collective-permute-done.11 = bf16[256,2048]{1,0:T(8,128)(2,1)S(1)} collective-permute-done((bf16[256,2048]{1,0:T(8,128)(2,1)S(1)}, bf16[256,2048]{1,0:T(8,128)(2,1)S(1)}, u32[]{:S(2)}, u32[]{:S(2)}) %collective-permute-start.11) | collective-permute-done | bytes 1048608 | tf_op jit(solution)/shard_map/ppermute | solution.py:14
  164.0 2.7 collective-permute-start.10
  167.8 2.7 collective-permute-start.13
  171.6 3.7 %collective-permute-done.5 = bf16[2048,128]{1,0:T(8,128)(2,1)S(1)} collective-permute-done((bf16[2048,128]{1,0:T(8,128)(2,1)S(1)}, bf16[2048,128]{1,0:T(8,128)(2,1)S(1)}, u32[]{:S(2)}, u32[]{:S(2)}) %collective-permute-start.5) | collective-permute-done | bytes 524320 | tf_op jit(solution)/shard_map/ppermute | solution.py:14
  175.3 2.8 collective-permute-start.14
  178.5 8.0 %collective-permute-done.9 = bf16[2048,128]{1,0:T(8,128)(2,1)S(1)} collective-permute-done((bf16[2048,128]{1,0:T(8,128)(2,1)S(1)}, bf16[2048,128]{1,0:T(8,128)(2,1)S(1)}, u32[]{:S(2)}, u32[]{:S(2)}) %collective-permute-start.9) | collective-permute-done | bytes 524320 | tf_op jit(solution)/shard_map/ppermute | solution.py:14
  186.7 2.0 collective-permute-done.10
  188.8 8.9 %collective-permute-done.13 = bf16[128,2048]{1,0:T(8,128)(2,1)S(1)} collective-permute-done((bf16[128,2048]{1,0:T(8,128)(2,1)S(1)}, bf16[128,2048]{1,0:T(8,128)(2,1)S(1)}, u32[]{:S(2)}, u32[]{:S(2)}) %collective-permute-start.13) | collective-permute-done | bytes 524320 | tf_op jit(solution)/shard_map/ppermute | solution.py:14
  198.5 1.3 collective-permute-done.14
  201.6 3.4 fusion.40
  205.0 5.9 %fusion = bf16[256,2048]{1,0:T(8,128)(2,1)S(1)} fusion(bf16[1024,2048]{1,0:T(8,128)(2,1)} %constant_dynamic-update-slice_fusion.10, f32[256]{0:T(256)S(1)} %select_reduce_fusion, bf16[256,2048]{1,0:T(8,128)(2,1)S(1)} %reshape.182, bf16[2048,1024]{1,0:T(8,128)(2,1)} %copy-done.2, f32[256,1024]{1,0:T(8,128)S(1)} %fusion.40), kind=kOutput, calls=%fused_computation.1 | convolution fusion | flops 2150105088 | bytes 11535360 | tf_op jit(solution)/shard_map/dot_general | solution.py:22
  211.4 132.6 %all_to_all.20 = bf16[64,4,2048]{2,1,0:T(4,128)(2,1)S(1)} all-to-all(bf16[64,4,2048]{2,1,0:T(4,128)(2,1)S(1)} %reshape.183), channel_id=1, replica_groups=mesh['cfg'=2,'expert_0'=32,'expert_1'=2,'ffn'=4] {'expert_0','expert_1'}, dimensions={0} | all-to-all | bytes 2097152 | tf_op jit(solution)/shard_map/all_to_all | solution.py:26
  345.9 3.6 all-to-all-start.3
  349.7 11.2 %all-to-all-done.3 = bf16[4,256,512]{2,1,0:T(8,128)(2,1)S(1)} async-done(((bf16[4,256,512]{2,1,0:T(8,128)(2,1)}), bf16[4,256,512]{2,1,0:T(8,128)(2,1)S(1)}, u32[]{:S(2)}, u32[]{:S(2)}) %all-to-all-start.3) | async-done | bytes 1048608 | tf_op jit(solution)/shard_map/all_to_all | solution.py:106
  (67 shorter events, 17.2 us)
Async XLA Ops:
  0.0 82.9 %collective-permute-start.2 = (bf16[256,512]{1,0:T(8,128)(2,1)}, bf16[256,512]{1,0:T(8,128)(2,1)S(1)}, u32[]{:S(2)}, u32[]{:S(2)}) collective-permute-start(bf16[256,512]{1,0:T(8,128)(2,1)} %param.7), channel_id=1, source_target_pairs={{0,3},{1,0},{2,1},{3,2},{4,7},{5,4},{6,5},{7,6},{8,11},{9,8},{10,9... | collective-permute-start | bytes 786440 | tf_op jit(solution)/shard_map/ppermute | solution.py:14
  5.6 77.2 %collective-permute-start.1 = (bf16[256,512]{1,0:T(8,128)(2,1)}, bf16[256,512]{1,0:T(8,128)(2,1)S(1)}, u32[]{:S(2)}, u32[]{:S(2)}) collective-permute-start(bf16[256,512]{1,0:T(8,128)(2,1)} %param.7), channel_id=1, source_target_pairs={{0,2},{1,3},{2,0},{3,1},{4,6},{5,7},{6,4},{7,5},{8,10},{9,11},{10,... | collective-permute-start | bytes 786440 | tf_op jit(solution)/shard_map/ppermute | solution.py:14
  7.8 75.0 %collective-permute-start = (bf16[256,512]{1,0:T(8,128)(2,1)}, bf16[256,512]{1,0:T(8,128)(2,1)S(1)}, u32[]{:S(2)}, u32[]{:S(2)}) collective-permute-start(bf16[256,512]{1,0:T(8,128)(2,1)} %param.7), channel_id=1, source_target_pairs={{0,1},{1,2},{2,3},{3,0},{4,5},{5,6},{6,7},{7,4},{8,9},{9,10},{10,1... | collective-permute-start | bytes 786440 | tf_op jit(solution)/shard_map/ppermute | solution.py:14
  13.3 69.3 %all-to-all-start = ((s32[64,1,16]{2,1,0:T(1,128)}), s32[64,1,16]{2,1,0:T(1,128)S(1)}, u32[]{:S(2)}, u32[]{:S(2)}) async-start(s32[64,1,16]{2,1,0:T(1,128)} %copy.22), calls=%async_computation | async-start | bytes 65536 | tf_op jit(solution)/shard_map/all_to_all | solution.py:26
  84.0 8.9 %copy-start.4 = (s32[1,512]{1,0:T(1,128)S(1)}, s32[1,512]{1,0:T(1,128)}, u32[]{:S(2)}) copy-start(s32[1,512]{1,0:T(1,128)} %param.8) | copy-start | bytes 6148
  84.0 8.9 %copy-start.1 = (bf16[1,2048,256]{2,1,0:T(8,128)(2,1)S(1)}, bf16[1,2048,256]{2,1,0:T(8,128)(2,1)}, u32[]{:S(2)}) copy-start(bf16[1,2048,256]{2,1,0:T(8,128)(2,1)} %param.11) | copy-start | bytes 3145732
  84.0 12.5 %copy-start.5 = (f32[1,512]{1,0:T(1,128)S(1)}, f32[1,512]{1,0:T(1,128)}, u32[]{:S(2)}) copy-start(f32[1,512]{1,0:T(1,128)} %param.9) | copy-start | bytes 6148
  85.3 22.5 %copy-start = (bf16[1,256,2048]{2,1,0:T(8,128)(2,1)S(1)}, bf16[1,256,2048]{2,1,0:T(8,128)(2,1)}, u32[]{:S(2)}) copy-start(bf16[1,256,2048]{2,1,0:T(8,128)(2,1)} %param.13) | copy-start | bytes 3145732
  86.5 114.8 %all-to-all-start.1 = ((bf16[64,4,2048]{2,1,0:T(4,128)(2,1)}), bf16[64,4,2048]{2,1,0:T(4,128)(2,1)S(1)}, u32[]{:S(2)}, u32[]{:S(2)}) async-start(bf16[64,4,2048]{2,1,0:T(4,128)(2,1)} %reshape.181), calls=%async_computation.1 | async-start | bytes 2097152 | tf_op jit(solution)/shard_map/all_to_all | solution.py:26
  92.9 26.2 %collective-permute-start.3 = (bf16[2048,256]{1,0:T(8,128)(2,1)S(1)}, bf16[2048,256]{1,0:T(8,128)(2,1)S(1)}, u32[]{:S(2)}, u32[]{:S(2)}) collective-permute-start(bf16[2048,256]{1,0:T(8,128)(2,1)S(1)} %bitcast.46), channel_id=1, source_target_pairs={{0,1},{1,2},{2,3},{3,0},{4,5},{5,6},{6,7},{7,4},{8,9},{9,10},{10,1... | collective-permute-start | bytes 3145736 | tf_op jit(solution)/shard_map/ppermute | solution.py:14
  96.5 25.4 %collective-permute-start.4 = (bf16[2048,256]{1,0:T(8,128)(2,1)S(1)}, bf16[2048,256]{1,0:T(8,128)(2,1)S(1)}, u32[]{:S(2)}, u32[]{:S(2)}) collective-permute-start(bf16[2048,256]{1,0:T(8,128)(2,1)S(1)} %bitcast.47), channel_id=1, source_target_pairs={{0,3},{1,0},{2,1},{3,2},{4,7},{5,4},{6,5},{7,6},{8,11},{9,8},{10,9... | collective-permute-start | bytes 3145736 | tf_op jit(solution)/shard_map/ppermute | solution.py:14
  99.5 42.1 %collective-permute-start.7 = (bf16[2048,256]{1,0:T(8,128)(2,1)}, bf16[2048,256]{1,0:T(8,128)(2,1)S(1)}, u32[]{:S(2)}, u32[]{:S(2)}) collective-permute-start(bf16[2048,256]{1,0:T(8,128)(2,1)} %bitcast.49), channel_id=1, source_target_pairs={{0,1},{1,2},{2,3},{3,0},{4,5},{5,6},{6,7},{7,4},{8,9},{9,10},{10,1... | collective-permute-start | bytes 3145736 | tf_op jit(solution)/shard_map/ppermute | solution.py:14
  102.1 42.5 %collective-permute-start.8 = (bf16[2048,256]{1,0:T(8,128)(2,1)}, bf16[2048,256]{1,0:T(8,128)(2,1)S(1)}, u32[]{:S(2)}, u32[]{:S(2)}) collective-permute-start(bf16[2048,256]{1,0:T(8,128)(2,1)} %bitcast.50), channel_id=1, source_target_pairs={{0,3},{1,0},{2,1},{3,2},{4,7},{5,4},{6,5},{7,6},{8,11},{9,8},{10,9... | collective-permute-start | bytes 3145736 | tf_op jit(solution)/shard_map/ppermute | solution.py:14
  107.8 56.2 %collective-permute-start.11 = (bf16[256,2048]{1,0:T(8,128)(2,1)S(1)}, bf16[256,2048]{1,0:T(8,128)(2,1)S(1)}, u32[]{:S(2)}, u32[]{:S(2)}) collective-permute-start(bf16[256,2048]{1,0:T(8,128)(2,1)S(1)} %bitcast.42), channel_id=1, source_target_pairs={{0,1},{1,2},{2,3},{3,0},{4,5},{5,6},{6,7},{7,4},{8,9},{9,10},{10,1... | collective-permute-start | bytes 3145736 | tf_op jit(solution)/shard_map/ppermute | solution.py:14
  119.1 48.7 %collective-permute-start.12 = (bf16[256,2048]{1,0:T(8,128)(2,1)S(1)}, bf16[256,2048]{1,0:T(8,128)(2,1)S(1)}, u32[]{:S(2)}, u32[]{:S(2)}) collective-permute-start(bf16[256,2048]{1,0:T(8,128)(2,1)S(1)} %bitcast.44), channel_id=1, source_target_pairs={{0,3},{1,0},{2,1},{3,2},{4,7},{5,4},{6,5},{7,6},{8,11},{9,8},{10,9... | collective-permute-start | bytes 3145736 | tf_op jit(solution)/shard_map/ppermute | solution.py:14
  121.9 53.3 %collective-permute-start.5 = (bf16[2048,128]{1,0:T(8,128)(2,1)S(1)}, bf16[2048,128]{1,0:T(8,128)(2,1)S(1)}, u32[]{:S(2)}, u32[]{:S(2)}) collective-permute-start(bf16[2048,128]{1,0:T(8,128)(2,1)S(1)} %slice.24), channel_id=1, source_target_pairs={{0,1},{1,2},{2,3},{3,0},{4,5},{5,6},{6,7},{7,4},{8,9},{9,10},{10,1... | collective-permute-start | bytes 1572872 | tf_op jit(solution)/shard_map/ppermute | solution.py:14
  141.6 36.7 %collective-permute-start.6 = (bf16[2048,128]{1,0:T(8,128)(2,1)S(1)}, bf16[2048,128]{1,0:T(8,128)(2,1)S(1)}, u32[]{:S(2)}, u32[]{:S(2)}) collective-permute-start(bf16[2048,128]{1,0:T(8,128)(2,1)S(1)} %slice.25), channel_id=1, source_target_pairs={{0,3},{1,0},{2,1},{3,2},{4,7},{5,4},{6,5},{7,6},{8,11},{9,8},{10,9... | collective-permute-start | bytes 1572872 | tf_op jit(solution)/shard_map/ppermute | solution.py:14
  144.6 41.9 %collective-permute-start.9 = (bf16[2048,128]{1,0:T(8,128)(2,1)S(1)}, bf16[2048,128]{1,0:T(8,128)(2,1)S(1)}, u32[]{:S(2)}, u32[]{:S(2)}) collective-permute-start(bf16[2048,128]{1,0:T(8,128)(2,1)S(1)} %slice.26), channel_id=1, source_target_pairs={{0,1},{1,2},{2,3},{3,0},{4,5},{5,6},{6,7},{7,4},{8,9},{9,10},{10,1... | collective-permute-start | bytes 1572872 | tf_op jit(solution)/shard_map/ppermute | solution.py:14
  164.0 24.6 %collective-permute-start.10 = (bf16[2048,128]{1,0:T(8,128)(2,1)S(1)}, bf16[2048,128]{1,0:T(8,128)(2,1)S(1)}, u32[]{:S(2)}, u32[]{:S(2)}) collective-permute-start(bf16[2048,128]{1,0:T(8,128)(2,1)S(1)} %slice.27), channel_id=1, source_target_pairs={{0,3},{1,0},{2,1},{3,2},{4,7},{5,4},{6,5},{7,6},{8,11},{9,8},{10,9... | collective-permute-start | bytes 1572872 | tf_op jit(solution)/shard_map/ppermute | solution.py:14
  167.8 29.9 %collective-permute-start.13 = (bf16[128,2048]{1,0:T(8,128)(2,1)S(1)}, bf16[128,2048]{1,0:T(8,128)(2,1)S(1)}, u32[]{:S(2)}, u32[]{:S(2)}) collective-permute-start(bf16[128,2048]{1,0:T(8,128)(2,1)S(1)} %slice.28), channel_id=1, source_target_pairs={{0,1},{1,2},{2,3},{3,0},{4,5},{5,6},{6,7},{7,4},{8,9},{9,10},{10,1... | collective-permute-start | bytes 1572872 | tf_op jit(solution)/shard_map/ppermute | solution.py:14
  175.3 24.6 %collective-permute-start.14 = (bf16[128,2048]{1,0:T(8,128)(2,1)S(1)}, bf16[128,2048]{1,0:T(8,128)(2,1)S(1)}, u32[]{:S(2)}, u32[]{:S(2)}) collective-permute-start(bf16[128,2048]{1,0:T(8,128)(2,1)S(1)} %slice.29), channel_id=1, source_target_pairs={{0,3},{1,0},{2,1},{3,2},{4,7},{5,4},{6,5},{7,6},{8,11},{9,8},{10,9... | collective-permute-start | bytes 1572872 | tf_op jit(solution)/shard_map/ppermute | solution.py:14
  178.5 21.4 %copy-start.3 = (bf16[2048,1024]{1,0:T(8,128)(2,1)}, bf16[2048,1024]{1,0:T(8,128)(2,1)S(1)}, u32[]{:S(2)}) copy-start(bf16[2048,1024]{1,0:T(8,128)(2,1)S(1)} %constant_dynamic-update-slice_fusion) | copy-start | bytes 12582916
  188.8 11.1 %copy-start.2 = (bf16[2048,1024]{1,0:T(8,128)(2,1)}, bf16[2048,1024]{1,0:T(8,128)(2,1)S(1)}, u32[]{:S(2)}) copy-start(bf16[2048,1024]{1,0:T(8,128)(2,1)S(1)} %constant_dynamic-update-slice_fusion.5) | copy-start | bytes 12582916
  345.9 15.1 %all-to-all-start.3 = ((bf16[4,256,512]{2,1,0:T(8,128)(2,1)}), bf16[4,256,512]{2,1,0:T(8,128)(2,1)S(1)}, u32[]{:S(2)}, u32[]{:S(2)}) async-start(bf16[4,256,512]{2,1,0:T(8,128)(2,1)} %copy.26), calls=%async_computation.3 | async-start | bytes 2097152 | tf_op jit(solution)/shard_map/all_to_all | solution.py:106

commit v2 on v1

--- a/solution.py
+++ b/solution.py
@@ -70,13 +70,16 @@
         ],
         axis=1,
     )
-    rows, shared = lax.optimization_barrier((rows, (w_gate[0], w_up[0], w_down[0])))
+    rows, own_down = lax.optimization_barrier((rows, w_down[0]))
     arrived = swap(rows.reshape(experts_n, depth, -1)).reshape(held, -1)
 
-    own_gate, _, _ = shared
+    own_gate, own_up = w_gate[0], w_up[0]
+    shared = [own_gate, own_up, own_down]
     half = own_gate.shape[1] // 2
-    left = [hop(w, 1) for w in shared]
-    right = [hop(w, -1) for w in shared]
+    left = [hop(own_gate, 1), hop(own_up, 1)]
+    right = [hop(own_gate, -1), hop(own_up, -1)]
+    left.append(hop(own_down, 1))
+    right.append(hop(own_down, -1))
     far_left = [hop(left[0][:, :half], 1), hop(left[1][:, :half], 1), hop(left[2][:half], 1)]
     far_right = [hop(right[0][:, half:], -1), hop(right[1][:, half:], -1), hop(right[2][half:], -1)]
 

time: 366 us -> 367 us (level)
  no operation moved by 1% of the time
where the time goes in v2:
time: 367 us; the launch traced here: 363 us
  blocking collectives  131 us (36%)
  starting transfers between devices  104 us (28%)
  waiting for transfers between devices  100 us (27%)
  matrix products  12.3 us (3%)
  local copies, waits for them, and re-layouts  11.7 us (3%)
    all_to_all x1, blocking collectives, swap(): lax.all_to_all(tiles, EXPERT, split_axis=0, concat_axis=0, tiled=True)  131 us
    ppermute x15, waiting for transfers between devices, hop(): lax.ppermute(array, 'ffn', [(k, (k + step) % peers) for k in range(peers)])  65.5 us
    all_to_all x2, starting transfers between devices, swap(): lax.all_to_all(tiles, EXPERT, split_axis=0, concat_axis=0, tiled=True)  53.7 us
    ppermute x15, starting transfers between devices, hop(): lax.ppermute(array, 'ffn', [(k, (k + step) % peers) for k in range(peers)])  45.1 us
    all_to_all x2, waiting for transfers between devices, swap(): lax.all_to_all(tiles, EXPERT, split_axis=0, concat_axis=0, tiled=True)  23.5 us
    dot_general x8, matrix products, mm(): return jnp.dot(a, b, preferred_element_type=jnp.float32)  11.9 us
    all_to_all x1, waiting for transfers between devices, shards(): lax.all_to_all(tiles, 'ffn', split_axis=0, concat_axis=0, tiled=True)  11.3 us
  transfers between devices with their start and end apart: 18, of which 11 were waited for; matrix products, arithmetic and copies ran while one was open for 3% of the time, Pallas kernels for 0%

profile of v2, /device:TPU:33, one launch (start us, length us, event | category | flops | bytes accessed | tf_op | source)
XLA Modules:
  0.0 362.8 jit_solution(1743336340853085140)
XLA Ops:
  0.0 5.8 %collective-permute-start.1 = (bf16[256,512]{1,0:T(8,128)(2,1)}, bf16[256,512]{1,0:T(8,128)(2,1)S(1)}, u32[]{:S(2)}, u32[]{:S(2)}) collective-permute-start(bf16[256,512]{1,0:T(8,128)(2,1)} %param.7), channel_id=1, source_target_pairs={{0,2},{1,3},{2,0},{3,1},{4,6},{5,7},{6,4},{7,5},{8,10},{9,11},{10,... | collective-permute-start | bytes 786440 | tf_op jit(solution)/shard_map/ppermute | solution.py:14
  5.8 2.7 collective-permute-start.2
  8.4 2.7 collective-permute-start
  13.9 47.5 %all-to-all-start = ((s32[64,1,16]{2,1,0:T(1,128)}), s32[64,1,16]{2,1,0:T(1,128)S(1)}, u32[]{:S(2)}, u32[]{:S(2)}) async-start(s32[64,1,16]{2,1,0:T(1,128)} %copy.22), calls=%async_computation | async-start | bytes 65536 | tf_op jit(solution)/shard_map/all_to_all | solution.py:26
  61.4 21.8 %all-to-all-done = s32[64,1,16]{2,1,0:T(1,128)S(1)} async-done(((s32[64,1,16]{2,1,0:T(1,128)}), s32[64,1,16]{2,1,0:T(1,128)S(1)}, u32[]{:S(2)}, u32[]{:S(2)}) %all-to-all-start) | async-done | bytes 4128 | tf_op jit(solution)/shard_map/all_to_all | solution.py:26
  85.9 1.2 reshape.181
  87.1 6.3 %all-to-all-start.1 = ((bf16[64,4,2048]{2,1,0:T(4,128)(2,1)}), bf16[64,4,2048]{2,1,0:T(4,128)(2,1)S(1)}, u32[]{:S(2)}, u32[]{:S(2)}) async-start(bf16[64,4,2048]{2,1,0:T(4,128)(2,1)} %reshape.181), calls=%async_computation.1 | async-start | bytes 2097152 | tf_op jit(solution)/shard_map/all_to_all | solution.py:26
  93.4 2.5 collective-permute-start.7
  96.0 4.2 %collective-permute-start.8 = (bf16[2048,256]{1,0:T(8,128)(2,1)S(1)}, bf16[2048,256]{1,0:T(8,128)(2,1)S(1)}, u32[]{:S(2)}, u32[]{:S(2)}) collective-permute-start(bf16[2048,256]{1,0:T(8,128)(2,1)S(1)} %bitcast.45), channel_id=1, source_target_pairs={{0,3},{1,0},{2,1},{3,2},{4,7},{5,4},{6,5},{7,6},{8,11},{9,8},{10,9... | collective-permute-start | bytes 3145736 | tf_op jit(solution)/shard_map/ppermute | solution.py:14
  100.1 2.0 collective-permute-start.3
  102.1 4.6 %collective-permute-start.4 = (bf16[2048,256]{1,0:T(8,128)(2,1)S(1)}, bf16[2048,256]{1,0:T(8,128)(2,1)S(1)}, u32[]{:S(2)}, u32[]{:S(2)}) collective-permute-start(bf16[2048,256]{1,0:T(8,128)(2,1)S(1)} %bitcast.47), channel_id=1, source_target_pairs={{0,3},{1,0},{2,1},{3,2},{4,7},{5,4},{6,5},{7,6},{8,11},{9,8},{10,9... | collective-permute-start | bytes 3145736 | tf_op jit(solution)/shard_map/ppermute | solution.py:14
  107.3 2.0 collective-permute-start.11
  110.4 9.4 %collective-permute-done.7 = bf16[2048,256]{1,0:T(8,128)(2,1)S(1)} collective-permute-done((bf16[2048,256]{1,0:T(8,128)(2,1)S(1)}, bf16[2048,256]{1,0:T(8,128)(2,1)S(1)}, u32[]{:S(2)}, u32[]{:S(2)}) %collective-permute-start.7) | collective-permute-done | bytes 1048608 | tf_op jit(solution)/shard_map/ppermute | solution.py:14
  119.8 2.7 collective-permute-start.12
  122.6 2.7 collective-permute-start.9
  125.4 16.9 %collective-permute-done.3 = bf16[2048,256]{1,0:T(8,128)(2,1)S(1)} collective-permute-done((bf16[2048,256]{1,0:T(8,128)(2,1)S(1)}, bf16[2048,256]{1,0:T(8,128)(2,1)S(1)}, u32[]{:S(2)}, u32[]{:S(2)}) %collective-permute-start.3) | collective-permute-done | bytes 1048608 | tf_op jit(solution)/shard_map/ppermute | solution.py:14
  142.2 2.7 collective-permute-start.10
  145.2 2.7 collective-permute-start.5
  148.1 16.6 %collective-permute-done.11 = bf16[256,2048]{1,0:T(8,128)(2,1)S(1)} collective-permute-done((bf16[256,2048]{1,0:T(8,128)(2,1)S(1)}, bf16[256,2048]{1,0:T(8,128)(2,1)S(1)}, u32[]{:S(2)}, u32[]{:S(2)}) %collective-permute-start.11) | collective-permute-done | bytes 1048608 | tf_op jit(solution)/shard_map/ppermute | solution.py:14
  164.7 2.7 collective-permute-start.6
  168.5 2.7 collective-permute-start.13
  172.3 3.7 %collective-permute-done.9 = bf16[2048,128]{1,0:T(8,128)(2,1)S(1)} collective-permute-done((bf16[2048,128]{1,0:T(8,128)(2,1)S(1)}, bf16[2048,128]{1,0:T(8,128)(2,1)S(1)}, u32[]{:S(2)}, u32[]{:S(2)}) %collective-permute-start.9) | collective-permute-done | bytes 524320 | tf_op jit(solution)/shard_map/ppermute | solution.py:14
  175.9 2.8 collective-permute-start.14
  179.2 8.0 %collective-permute-done.5 = bf16[2048,128]{1,0:T(8,128)(2,1)S(1)} collective-permute-done((bf16[2048,128]{1,0:T(8,128)(2,1)S(1)}, bf16[2048,128]{1,0:T(8,128)(2,1)S(1)}, u32[]{:S(2)}, u32[]{:S(2)}) %collective-permute-start.5) | collective-permute-done | bytes 524320 | tf_op jit(solution)/shard_map/ppermute | solution.py:14
  188.3 10.1 %collective-permute-done.13 = bf16[128,2048]{1,0:T(8,128)(2,1)S(1)} collective-permute-done((bf16[128,2048]{1,0:T(8,128)(2,1)S(1)}, bf16[128,2048]{1,0:T(8,128)(2,1)S(1)}, u32[]{:S(2)}, u32[]{:S(2)}) %collective-permute-start.13) | collective-permute-done | bytes 524320 | tf_op jit(solution)/shard_map/ppermute | solution.py:14
  200.2 1.7 all-to-all-done.1
  202.2 3.4 fusion.40
  205.6 5.9 %fusion = bf16[256,2048]{1,0:T(8,128)(2,1)S(1)} fusion(bf16[1024,2048]{1,0:T(8,128)(2,1)} %constant_dynamic-update-slice_fusion.10, f32[256]{0:T(256)S(1)} %select_reduce_fusion, bf16[256,2048]{1,0:T(8,128)(2,1)S(1)} %reshape.182, bf16[2048,1024]{1,0:T(8,128)(2,1)} %copy-done.4, f32[256,1024]{1,0:T(8,128)S(1)} %fusion.40), kind=kOutput, calls=%fused_computation.1 | convolution fusion | flops 2150105088 | bytes 11535360 | tf_op jit(solution)/shard_map/dot_general | solution.py:22
  212.0 131.5 %all_to_all.20 = bf16[64,4,2048]{2,1,0:T(4,128)(2,1)S(1)} all-to-all(bf16[64,4,2048]{2,1,0:T(4,128)(2,1)S(1)} %reshape.183), channel_id=1, replica_groups=mesh['cfg'=2,'expert_0'=32,'expert_1'=2,'ffn'=4] {'expert_0','expert_1'}, dimensions={0} | all-to-all | bytes 2097152 | tf_op jit(solution)/shard_map/all_to_all | solution.py:26
  344.2 1.2 copy.26
  345.4 4.7 %all-to-all-start.3 = ((bf16[4,256,512]{2,1,0:T(8,128)(2,1)}), bf16[4,256,512]{2,1,0:T(8,128)(2,1)S(1)}, u32[]{:S(2)}, u32[]{:S(2)}) async-start(bf16[4,256,512]{2,1,0:T(8,128)(2,1)} %copy.26), calls=%async_computation.3 | async-start | bytes 2097152 | tf_op jit(solution)/shard_map/all_to_all | solution.py:109
  350.3 11.3 %all-to-all-done.3 = bf16[4,256,512]{2,1,0:T(8,128)(2,1)S(1)} async-done(((bf16[4,256,512]{2,1,0:T(8,128)(2,1)}), bf16[4,256,512]{2,1,0:T(8,128)(2,1)S(1)}, u32[]{:S(2)}, u32[]{:S(2)}) %all-to-all-start.3) | async-done | bytes 1048608 | tf_op jit(solution)/shard_map/all_to_all | solution.py:109
  (70 shorter events, 15.3 us)
Async XLA Ops:
  0.0 83.5 %collective-permute-start.1 = (bf16[256,512]{1,0:T(8,128)(2,1)}, bf16[256,512]{1,0:T(8,128)(2,1)S(1)}, u32[]{:S(2)}, u32[]{:S(2)}) collective-permute-start(bf16[256,512]{1,0:T(8,128)(2,1)} %param.7), channel_id=1, source_target_pairs={{0,2},{1,3},{2,0},{3,1},{4,6},{5,7},{6,4},{7,5},{8,10},{9,11},{10,... | collective-permute-start | bytes 786440 | tf_op jit(solution)/shard_map/ppermute | solution.py:14
  5.8 77.7 %collective-permute-start.2 = (bf16[256,512]{1,0:T(8,128)(2,1)}, bf16[256,512]{1,0:T(8,128)(2,1)S(1)}, u32[]{:S(2)}, u32[]{:S(2)}) collective-permute-start(bf16[256,512]{1,0:T(8,128)(2,1)} %param.7), channel_id=1, source_target_pairs={{0,3},{1,0},{2,1},{3,2},{4,7},{5,4},{6,5},{7,6},{8,11},{9,8},{10,9... | collective-permute-start | bytes 786440 | tf_op jit(solution)/shard_map/ppermute | solution.py:14
  8.4 75.0 %collective-permute-start = (bf16[256,512]{1,0:T(8,128)(2,1)}, bf16[256,512]{1,0:T(8,128)(2,1)S(1)}, u32[]{:S(2)}, u32[]{:S(2)}) collective-permute-start(bf16[256,512]{1,0:T(8,128)(2,1)} %param.7), channel_id=1, source_target_pairs={{0,1},{1,2},{2,3},{3,0},{4,5},{5,6},{6,7},{7,4},{8,9},{9,10},{10,1... | collective-permute-start | bytes 786440 | tf_op jit(solution)/shard_map/ppermute | solution.py:14
  13.9 69.3 %all-to-all-start = ((s32[64,1,16]{2,1,0:T(1,128)}), s32[64,1,16]{2,1,0:T(1,128)S(1)}, u32[]{:S(2)}, u32[]{:S(2)}) async-start(s32[64,1,16]{2,1,0:T(1,128)} %copy.22), calls=%async_computation | async-start | bytes 65536 | tf_op jit(solution)/shard_map/all_to_all | solution.py:26
  84.6 8.9 %copy-start = (bf16[1,2048,256]{2,1,0:T(8,128)(2,1)S(1)}, bf16[1,2048,256]{2,1,0:T(8,128)(2,1)}, u32[]{:S(2)}) copy-start(bf16[1,2048,256]{2,1,0:T(8,128)(2,1)} %param.12) | copy-start | bytes 3145732
  84.6 15.6 %copy-start.1 = (bf16[1,2048,256]{2,1,0:T(8,128)(2,1)S(1)}, bf16[1,2048,256]{2,1,0:T(8,128)(2,1)}, u32[]{:S(2)}) copy-start(bf16[1,2048,256]{2,1,0:T(8,128)(2,1)} %param.11) | copy-start | bytes 3145732
  84.6 22.1 %copy-start.6 = (f32[1,512]{1,0:T(1,128)S(1)}, f32[1,512]{1,0:T(1,128)}, u32[]{:S(2)}) copy-start(f32[1,512]{1,0:T(1,128)} %param.9) | copy-start | bytes 6148
  84.6 22.1 %copy-start.5 = (s32[1,512]{1,0:T(1,128)S(1)}, s32[1,512]{1,0:T(1,128)}, u32[]{:S(2)}) copy-start(s32[1,512]{1,0:T(1,128)} %param.8) | copy-start | bytes 6148
  87.1 114.8 %all-to-all-start.1 = ((bf16[64,4,2048]{2,1,0:T(4,128)(2,1)}), bf16[64,4,2048]{2,1,0:T(4,128)(2,1)S(1)}, u32[]{:S(2)}, u32[]{:S(2)}) async-start(bf16[64,4,2048]{2,1,0:T(4,128)(2,1)} %reshape.181), calls=%async_computation.1 | async-start | bytes 2097152 | tf_op jit(solution)/shard_map/all_to_all | solution.py:26
  93.4 13.9 %copy-start.2 = (bf16[1,256,2048]{2,1,0:T(8,128)(2,1)S(1)}, bf16[1,256,2048]{2,1,0:T(8,128)(2,1)}, u32[]{:S(2)}) copy-start(bf16[1,256,2048]{2,1,0:T(8,128)(2,1)} %param.13) | copy-start | bytes 3145732
  93.4 26.3 %collective-permute-start.7 = (bf16[2048,256]{1,0:T(8,128)(2,1)S(1)}, bf16[2048,256]{1,0:T(8,128)(2,1)S(1)}, u32[]{:S(2)}, u32[]{:S(2)}) collective-permute-start(bf16[2048,256]{1,0:T(8,128)(2,1)S(1)} %bitcast.44), channel_id=1, source_target_pairs={{0,1},{1,2},{2,3},{3,0},{4,5},{5,6},{6,7},{7,4},{8,9},{9,10},{10,1... | collective-permute-start | bytes 3145736 | tf_op jit(solution)/shard_map/ppermute | solution.py:14
  96.0 26.7 %collective-permute-start.8 = (bf16[2048,256]{1,0:T(8,128)(2,1)S(1)}, bf16[2048,256]{1,0:T(8,128)(2,1)S(1)}, u32[]{:S(2)}, u32[]{:S(2)}) collective-permute-start(bf16[2048,256]{1,0:T(8,128)(2,1)S(1)} %bitcast.45), channel_id=1, source_target_pairs={{0,3},{1,0},{2,1},{3,2},{4,7},{5,4},{6,5},{7,6},{8,11},{9,8},{10,9... | collective-permute-start | bytes 3145736 | tf_op jit(solution)/shard_map/ppermute | solution.py:14
  100.1 42.1 %collective-permute-start.3 = (bf16[2048,256]{1,0:T(8,128)(2,1)S(1)}, bf16[2048,256]{1,0:T(8,128)(2,1)S(1)}, u32[]{:S(2)}, u32[]{:S(2)}) collective-permute-start(bf16[2048,256]{1,0:T(8,128)(2,1)S(1)} %bitcast.46), channel_id=1, source_target_pairs={{0,1},{1,2},{2,3},{3,0},{4,5},{5,6},{6,7},{7,4},{8,9},{9,10},{10,1... | collective-permute-start | bytes 3145736 | tf_op jit(solution)/shard_map/ppermute | solution.py:14
  102.1 43.1 %collective-permute-start.4 = (bf16[2048,256]{1,0:T(8,128)(2,1)S(1)}, bf16[2048,256]{1,0:T(8,128)(2,1)S(1)}, u32[]{:S(2)}, u32[]{:S(2)}) collective-permute-start(bf16[2048,256]{1,0:T(8,128)(2,1)S(1)} %bitcast.47), channel_id=1, source_target_pairs={{0,3},{1,0},{2,1},{3,2},{4,7},{5,4},{6,5},{7,6},{8,11},{9,8},{10,9... | collective-permute-start | bytes 3145736 | tf_op jit(solution)/shard_map/ppermute | solution.py:14
  107.3 57.4 %collective-permute-start.11 = (bf16[256,2048]{1,0:T(8,128)(2,1)S(1)}, bf16[256,2048]{1,0:T(8,128)(2,1)S(1)}, u32[]{:S(2)}, u32[]{:S(2)}) collective-permute-start(bf16[256,2048]{1,0:T(8,128)(2,1)S(1)} %bitcast.48), channel_id=1, source_target_pairs={{0,1},{1,2},{2,3},{3,0},{4,5},{5,6},{6,7},{7,4},{8,9},{9,10},{10,1... | collective-permute-start | bytes 3145736 | tf_op jit(solution)/shard_map/ppermute | solution.py:14
  119.8 48.7 %collective-permute-start.12 = (bf16[256,2048]{1,0:T(8,128)(2,1)S(1)}, bf16[256,2048]{1,0:T(8,128)(2,1)S(1)}, u32[]{:S(2)}, u32[]{:S(2)}) collective-permute-start(bf16[256,2048]{1,0:T(8,128)(2,1)S(1)} %bitcast.50), channel_id=1, source_target_pairs={{0,3},{1,0},{2,1},{3,2},{4,7},{5,4},{6,5},{7,6},{8,11},{9,8},{10,9... | collective-permute-start | bytes 3145736 | tf_op jit(solution)/shard_map/ppermute | solution.py:14
  122.6 53.3 %collective-permute-start.9 = (bf16[2048,128]{1,0:T(8,128)(2,1)S(1)}, bf16[2048,128]{1,0:T(8,128)(2,1)S(1)}, u32[]{:S(2)}, u32[]{:S(2)}) collective-permute-start(bf16[2048,128]{1,0:T(8,128)(2,1)S(1)} %slice.26), channel_id=1, source_target_pairs={{0,1},{1,2},{2,3},{3,0},{4,5},{5,6},{6,7},{7,4},{8,9},{9,10},{10,1... | collective-permute-start | bytes 1572872 | tf_op jit(solution)/shard_map/ppermute | solution.py:14
  142.2 36.7 %collective-permute-start.10 = (bf16[2048,128]{1,0:T(8,128)(2,1)S(1)}, bf16[2048,128]{1,0:T(8,128)(2,1)S(1)}, u32[]{:S(2)}, u32[]{:S(2)}) collective-permute-start(bf16[2048,128]{1,0:T(8,128)(2,1)S(1)} %slice.27), channel_id=1, source_target_pairs={{0,3},{1,0},{2,1},{3,2},{4,7},{5,4},{6,5},{7,6},{8,11},{9,8},{10,9... | collective-permute-start | bytes 1572872 | tf_op jit(solution)/shard_map/ppermute | solution.py:14
  145.2 41.9 %collective-permute-start.5 = (bf16[2048,128]{1,0:T(8,128)(2,1)S(1)}, bf16[2048,128]{1,0:T(8,128)(2,1)S(1)}, u32[]{:S(2)}, u32[]{:S(2)}) collective-permute-start(bf16[2048,128]{1,0:T(8,128)(2,1)S(1)} %slice.24), channel_id=1, source_target_pairs={{0,1},{1,2},{2,3},{3,0},{4,5},{5,6},{6,7},{7,4},{8,9},{9,10},{10,1... | collective-permute-start | bytes 1572872 | tf_op jit(solution)/shard_map/ppermute | solution.py:14
  164.7 23.4 %collective-permute-start.6 = (bf16[2048,128]{1,0:T(8,128)(2,1)S(1)}, bf16[2048,128]{1,0:T(8,128)(2,1)S(1)}, u32[]{:S(2)}, u32[]{:S(2)}) collective-permute-start(bf16[2048,128]{1,0:T(8,128)(2,1)S(1)} %slice.25), channel_id=1, source_target_pairs={{0,3},{1,0},{2,1},{3,2},{4,7},{5,4},{6,5},{7,6},{8,11},{9,8},{10,9... | collective-permute-start | bytes 1572872 | tf_op jit(solution)/shard_map/ppermute | solution.py:14
  168.5 29.9 %collective-permute-start.13 = (bf16[128,2048]{1,0:T(8,128)(2,1)S(1)}, bf16[128,2048]{1,0:T(8,128)(2,1)S(1)}, u32[]{:S(2)}, u32[]{:S(2)}) collective-permute-start(bf16[128,2048]{1,0:T(8,128)(2,1)S(1)} %slice.28), channel_id=1, source_target_pairs={{0,1},{1,2},{2,3},{3,0},{4,5},{5,6},{6,7},{7,4},{8,9},{9,10},{10,1... | collective-permute-start | bytes 1572872 | tf_op jit(solution)/shard_map/ppermute | solution.py:14
  175.9 23.4 %collective-permute-start.14 = (bf16[128,2048]{1,0:T(8,128)(2,1)S(1)}, bf16[128,2048]{1,0:T(8,128)(2,1)S(1)}, u32[]{:S(2)}, u32[]{:S(2)}) collective-permute-start(bf16[128,2048]{1,0:T(8,128)(2,1)S(1)} %slice.29), channel_id=1, source_target_pairs={{0,3},{1,0},{2,1},{3,2},{4,7},{5,4},{6,5},{7,6},{8,11},{9,8},{10,9... | collective-permute-start | bytes 1572872 | tf_op jit(solution)/shard_map/ppermute | solution.py:14
  179.2 20.2 %copy-start.4 = (bf16[2048,1024]{1,0:T(8,128)(2,1)}, bf16[2048,1024]{1,0:T(8,128)(2,1)S(1)}, u32[]{:S(2)}) copy-start(bf16[2048,1024]{1,0:T(8,128)(2,1)S(1)} %constant_dynamic-update-slice_fusion.5) | copy-start | bytes 12582916
  188.3 11.1 %copy-start.3 = (bf16[2048,1024]{1,0:T(8,128)(2,1)}, bf16[2048,1024]{1,0:T(8,128)(2,1)S(1)}, u32[]{:S(2)}) copy-start(bf16[2048,1024]{1,0:T(8,128)(2,1)S(1)} %constant_dynamic-update-slice_fusion) | copy-start | bytes 12582916
  345.4 16.2 %all-to-all-start.3 = ((bf16[4,256,512]{2,1,0:T(8,128)(2,1)}), bf16[4,256,512]{2,1,0:T(8,128)(2,1)S(1)}, u32[]{:S(2)}, u32[]{:S(2)}) async-start(bf16[4,256,512]{2,1,0:T(8,128)(2,1)} %copy.26), calls=%async_computation.3 | async-start | bytes 2097152 | tf_op jit(solution)/shard_map/all_to_all | solution.py:109

commit v3 on v2

--- a/solution.py
+++ b/solution.py
@@ -75,13 +75,10 @@
 
     own_gate, own_up = w_gate[0], w_up[0]
     shared = [own_gate, own_up, own_down]
-    half = own_gate.shape[1] // 2
-    left = [hop(own_gate, 1), hop(own_up, 1)]
-    right = [hop(own_gate, -1), hop(own_up, -1)]
-    left.append(hop(own_down, 1))
-    right.append(hop(own_down, -1))
-    far_left = [hop(left[0][:, :half], 1), hop(left[1][:, :half], 1), hop(left[2][:half], 1)]
-    far_right = [hop(right[0][:, half:], -1), hop(right[1][:, half:], -1), hop(right[2][half:], -1)]
+    right_gate, right_up = hop(own_gate, -1), hop(own_up, -1)
+    left = [hop(own_gate, 1), hop(own_up, 1), hop(own_down, 1)]
+    right = [right_gate, right_up, hop(own_down, -1)]
+    far = [hop(left[0], 1), hop(right[1], -1), hop(right[2], -1)]
 
     slot_of = source * depth + rank_in // ffn_n
     at_mine = (rank_in % ffn_n) == me
@@ -97,7 +94,7 @@
 
     joined = []
     for k, dim in ((0, 1), (1, 1), (2, 0)):
-        parts = [g[k] for g in (shared, left, right, far_left, far_right)]
+        parts = [g[k] for g in (shared, left, right, far)]
         joined.append(jnp.concatenate(parts, axis=dim))
     gate_cols, up_cols, down_rows = lax.optimization_barrier(tuple(joined))
     hidden = (jax.nn.silu(mm(arrived, gate_cols)) * mm(arrived, up_cols)).astype(jnp.bfloat16)

time: 367 us -> 379 us (1.033)
  waiting for transfers between devices: 100 us -> 118 us
  starting transfers between devices: 104 us -> 96.3 us
  other arithmetic: 2.16 us -> 8.95 us
  local copies, waits for them, and re-layouts: 11.7 us -> 5.05 us
    ppermute x15 -> x12, waiting for transfers between devices: 65.5 us -> 85.4 us  [hop(): lax.ppermute(array, 'ffn', [(k, (k + step) % peers) for k in range(peers)])]
    ppermute x15 -> x12, starting transfers between devices: 45.1 us -> 37.8 us  [hop(): lax.ppermute(array, 'ffn', [(k, (k + step) % peers) for k in range(peers)])]
    concatenate x0 -> x3, other arithmetic: none -> 6.8 us  [shards(): joined.append(jnp.concatenate(parts, axis=dim))]
    unnamed x26 -> x10, local copies, waits for them, and re-layouts: 5.26 us -> 0.03 us
  transfers between devices with their start and end apart: 18 -> 15, of which waited for: 11 -> 7; matrix products, arithmetic and copies ran while one was open for 3% -> 3% of each run, Pallas kernels for 0% -> 0%
where the time goes in v3:
time: 379 us; the launch traced here: 375 us
  blocking collectives  133 us (35%)
  waiting for transfers between devices  118 us (31%)
  starting transfers between devices  96.3 us (25%)
  matrix products  12.3 us (3%)
  other arithmetic  8.95 us (2%)
  local copies, waits for them, and re-layouts  5.05 us (1%)
    all_to_all x1, blocking collectives, swap(): lax.all_to_all(tiles, EXPERT, split_axis=0, concat_axis=0, tiled=True)  133 us
    ppermute x12, waiting for transfers between devices, hop(): lax.ppermute(array, 'ffn', [(k, (k + step) % peers) for k in range(peers)])  85.4 us
    all_to_all x2, starting transfers between devices, swap(): lax.all_to_all(tiles, EXPERT, split_axis=0, concat_axis=0, tiled=True)  53.7 us
    ppermute x12, starting transfers between devices, hop(): lax.ppermute(array, 'ffn', [(k, (k + step) % peers) for k in range(peers)])  37.8 us
    all_to_all x2, waiting for transfers between devices, swap(): lax.all_to_all(tiles, EXPERT, split_axis=0, concat_axis=0, tiled=True)  21.8 us
    dot_general x8, matrix products, mm(): return jnp.dot(a, b, preferred_element_type=jnp.float32)  11.9 us
    all_to_all x1, waiting for transfers between devices, shards(): lax.all_to_all(tiles, 'ffn', split_axis=0, concat_axis=0, tiled=True)  11.3 us
  transfers between devices with their start and end apart: 15, of which 7 were waited for; matrix products, arithmetic and copies ran while one was open for 3% of the time, Pallas kernels for 0%

profile of v3, /device:TPU:33, one launch (start us, length us, event | category | flops | bytes accessed | tf_op | source)
XLA Modules:
  0.0 375.4 jit_solution(9817157135058837901)
XLA Ops:
  0.0 4.1 %collective-permute-start = (bf16[256,512]{1,0:T(8,128)(2,1)}, bf16[256,512]{1,0:T(8,128)(2,1)S(1)}, u32[]{:S(2)}, u32[]{:S(2)}) collective-permute-start(bf16[256,512]{1,0:T(8,128)(2,1)} %param.7), channel_id=1, source_target_pairs={{0,1},{1,2},{2,3},{3,0},{4,5},{5,6},{6,7},{7,4},{8,9},{9,10},{10,1... | collective-permute-start | bytes 786440 | tf_op jit(solution)/shard_map/ppermute | solution.py:14
  4.1 3.5 collective-permute-start.2
  7.6 3.5 collective-permute-start.1
  13.9 47.5 %all-to-all-start = ((s32[64,1,16]{2,1,0:T(1,128)}), s32[64,1,16]{2,1,0:T(1,128)S(1)}, u32[]{:S(2)}, u32[]{:S(2)}) async-start(s32[64,1,16]{2,1,0:T(1,128)} %copy.22), calls=%async_computation | async-start | bytes 65536 | tf_op jit(solution)/shard_map/all_to_all | solution.py:26
  61.4 21.8 %all-to-all-done = s32[64,1,16]{2,1,0:T(1,128)S(1)} async-done(((s32[64,1,16]{2,1,0:T(1,128)}), s32[64,1,16]{2,1,0:T(1,128)S(1)}, u32[]{:S(2)}, u32[]{:S(2)}) %all-to-all-start) | async-done | bytes 4128 | tf_op jit(solution)/shard_map/all_to_all | solution.py:26
  83.5 1.1 pad_maximum_fusion.3
  85.9 1.2 reshape.181
  87.1 6.3 %all-to-all-start.1 = ((bf16[64,4,2048]{2,1,0:T(4,128)(2,1)}), bf16[64,4,2048]{2,1,0:T(4,128)(2,1)S(1)}, u32[]{:S(2)}, u32[]{:S(2)}) async-start(bf16[64,4,2048]{2,1,0:T(4,128)(2,1)} %reshape.181), calls=%async_computation.1 | async-start | bytes 2097152 | tf_op jit(solution)/shard_map/all_to_all | solution.py:26
  93.4 2.4 collective-permute-start.3
  95.8 4.2 %collective-permute-start.7 = (bf16[2048,256]{1,0:T(8,128)(2,1)S(1)}, bf16[2048,256]{1,0:T(8,128)(2,1)S(1)}, u32[]{:S(2)}, u32[]{:S(2)}) collective-permute-start(bf16[2048,256]{1,0:T(8,128)(2,1)S(1)} %bitcast.46), channel_id=1, source_target_pairs={{0,3},{1,0},{2,1},{3,2},{4,7},{5,4},{6,5},{7,6},{8,11},{9,8},{10,9... | collective-permute-start | bytes 3145736 | tf_op jit(solution)/shard_map/ppermute | solution.py:14
  100.0 2.0 collective-permute-start.4
  102.0 2.2 collective-permute-start.10
  104.1 15.5 %collective-permute-done.3 = bf16[2048,256]{1,0:T(8,128)(2,1)S(1)} collective-permute-done((bf16[2048,256]{1,0:T(8,128)(2,1)S(1)}, bf16[2048,256]{1,0:T(8,128)(2,1)S(1)}, u32[]{:S(2)}, u32[]{:S(2)}) %collective-permute-start.3) | collective-permute-done | bytes 1048608 | tf_op jit(solution)/shard_map/ppermute | solution.py:14
  119.6 1.9 collective-permute-start.5
  121.6 2.0 collective-permute-start.6
  123.5 4.6 %collective-permute-start.8 = (bf16[2048,256]{1,0:T(8,128)(2,1)S(1)}, bf16[2048,256]{1,0:T(8,128)(2,1)S(1)}, u32[]{:S(2)}, u32[]{:S(2)}) collective-permute-start(bf16[2048,256]{1,0:T(8,128)(2,1)S(1)} %collective-permute-done.7), channel_id=1, source_target_pairs={{0,3},{1,0},{2,1},{3,2},{4,7},{5,4},{6,5},{7,6},{8,11},{9,8},{10,9... | collective-permute-start | bytes 3145736 | tf_op jit(solution)/shard_map/ppermute | solution.py:14
  128.2 14.8 %collective-permute-done.4 = bf16[2048,256]{1,0:T(8,128)(2,1)S(1)} collective-permute-done((bf16[2048,256]{1,0:T(8,128)(2,1)S(1)}, bf16[2048,256]{1,0:T(8,128)(2,1)S(1)}, u32[]{:S(2)}, u32[]{:S(2)}) %collective-permute-start.4) | collective-permute-done | bytes 1048608 | tf_op jit(solution)/shard_map/ppermute | solution.py:14
  143.0 2.3 collective-permute-start.9
  145.3 20.3 %collective-permute-done.10 = bf16[256,2048]{1,0:T(8,128)(2,1)S(1)} collective-permute-done((bf16[256,2048]{1,0:T(8,128)(2,1)}, bf16[256,2048]{1,0:T(8,128)(2,1)S(1)}, u32[]{:S(2)}, u32[]{:S(2)}) %collective-permute-start.10) | collective-permute-done | bytes 1048608 | tf_op jit(solution)/shard_map/ppermute | solution.py:14
  165.6 5.2 %collective-permute-start.11 = (bf16[256,2048]{1,0:T(8,128)(2,1)S(1)}, bf16[256,2048]{1,0:T(8,128)(2,1)S(1)}, u32[]{:S(2)}, u32[]{:S(2)}) collective-permute-start(bf16[256,2048]{1,0:T(8,128)(2,1)S(1)} %collective-permute-done.10), channel_id=1, source_target_pairs={{0,3},{1,0},{2,1},{3,2},{4,7},{5,4},{6,5},{7,6},{8,11},{9,8},{10,9... | collective-permute-start | bytes 3145736 | tf_op jit(solution)/shard_map/ppermute | solution.py:14
  171.1 2.3 pad_maximum_fusion
  173.3 14.6 %collective-permute-done.8 = bf16[2048,256]{1,0:T(8,128)(2,1)S(1)} collective-permute-done((bf16[2048,256]{1,0:T(8,128)(2,1)S(1)}, bf16[2048,256]{1,0:T(8,128)(2,1)S(1)}, u32[]{:S(2)}, u32[]{:S(2)}) %collective-permute-start.8) | collective-permute-done | bytes 1048608 | tf_op jit(solution)/shard_map/ppermute | solution.py:14
  188.0 2.3 pad_maximum_fusion.1
  190.3 20.2 %collective-permute-done.11 = bf16[256,2048]{1,0:T(8,128)(2,1)S(1)} collective-permute-done((bf16[256,2048]{1,0:T(8,128)(2,1)S(1)}, bf16[256,2048]{1,0:T(8,128)(2,1)S(1)}, u32[]{:S(2)}, u32[]{:S(2)}) %collective-permute-start.11) | collective-permute-done | bytes 1048608 | tf_op jit(solution)/shard_map/ppermute | solution.py:14
  210.4 2.2 pad_maximum_fusion.2
  213.0 3.4 fusion.40
  216.4 5.9 %fusion = bf16[256,2048]{1,0:T(8,128)(2,1)S(1)} fusion(bf16[1024,2048]{1,0:T(8,128)(2,1)} %pad_maximum_fusion.2, f32[256]{0:T(256)S(1)} %select_reduce_fusion, bf16[256,2048]{1,0:T(8,128)(2,1)S(1)} %reshape.182, bf16[2048,1024]{1,0:T(8,128)(2,1)} %pad_maximum_fusion.1, f32[256,1024]{1,0:T(8,128)S(1)} %fusion.40), kind=kOutput, calls=%fused_computation.4 | convolution fusion | flops 2150105088 | bytes 11535360 | tf_op jit(solution)/shard_map/dot_general | solution.py:22
  222.8 133.4 %all_to_all.20 = bf16[64,4,2048]{2,1,0:T(4,128)(2,1)S(1)} all-to-all(bf16[64,4,2048]{2,1,0:T(4,128)(2,1)S(1)} %reshape.183), channel_id=1, replica_groups=mesh['cfg'=2,'expert_0'=32,'expert_1'=2,'ffn'=4] {'expert_0','expert_1'}, dimensions={0} | all-to-all | bytes 2097152 | tf_op jit(solution)/shard_map/all_to_all | solution.py:26
  356.8 1.2 copy.26
  358.0 4.7 %all-to-all-start.3 = ((bf16[4,256,512]{2,1,0:T(8,128)(2,1)}), bf16[4,256,512]{2,1,0:T(8,128)(2,1)S(1)}, u32[]{:S(2)}, u32[]{:S(2)}) async-start(bf16[4,256,512]{2,1,0:T(8,128)(2,1)} %copy.26), calls=%async_computation.3 | async-start | bytes 2097152 | tf_op jit(solution)/shard_map/all_to_all | solution.py:106
  362.9 11.3 %all-to-all-done.3 = bf16[4,256,512]{2,1,0:T(8,128)(2,1)S(1)} async-done(((bf16[4,256,512]{2,1,0:T(8,128)(2,1)}), bf16[4,256,512]{2,1,0:T(8,128)(2,1)S(1)}, u32[]{:S(2)}, u32[]{:S(2)}) %all-to-all-start.3) | async-done | bytes 1048608 | tf_op jit(solution)/shard_map/all_to_all | solution.py:106
  374.3 1.2 convolution_convert_fusion
  (42 shorter events, 5.5 us)
Async XLA Ops:
  0.0 83.5 %collective-permute-start = (bf16[256,512]{1,0:T(8,128)(2,1)}, bf16[256,512]{1,0:T(8,128)(2,1)S(1)}, u32[]{:S(2)}, u32[]{:S(2)}) collective-permute-start(bf16[256,512]{1,0:T(8,128)(2,1)} %param.7), channel_id=1, source_target_pairs={{0,1},{1,2},{2,3},{3,0},{4,5},{5,6},{6,7},{7,4},{8,9},{9,10},{10,1... | collective-permute-start | bytes 786440 | tf_op jit(solution)/shard_map/ppermute | solution.py:14
  4.1 79.4 %collective-permute-start.2 = (bf16[256,512]{1,0:T(8,128)(2,1)}, bf16[256,512]{1,0:T(8,128)(2,1)S(1)}, u32[]{:S(2)}, u32[]{:S(2)}) collective-permute-start(bf16[256,512]{1,0:T(8,128)(2,1)} %param.7), channel_id=1, source_target_pairs={{0,3},{1,0},{2,1},{3,2},{4,7},{5,4},{6,5},{7,6},{8,11},{9,8},{10,9... | collective-permute-start | bytes 786440 | tf_op jit(solution)/shard_map/ppermute | solution.py:14
  7.6 75.9 %collective-permute-start.1 = (bf16[256,512]{1,0:T(8,128)(2,1)}, bf16[256,512]{1,0:T(8,128)(2,1)S(1)}, u32[]{:S(2)}, u32[]{:S(2)}) collective-permute-start(bf16[256,512]{1,0:T(8,128)(2,1)} %param.7), channel_id=1, source_target_pairs={{0,2},{1,3},{2,0},{3,1},{4,6},{5,7},{6,4},{7,5},{8,10},{9,11},{10,... | collective-permute-start | bytes 786440 | tf_op jit(solution)/shard_map/ppermute | solution.py:14
  13.9 69.3 %all-to-all-start = ((s32[64,1,16]{2,1,0:T(1,128)}), s32[64,1,16]{2,1,0:T(1,128)S(1)}, u32[]{:S(2)}, u32[]{:S(2)}) async-start(s32[64,1,16]{2,1,0:T(1,128)} %copy.22), calls=%async_computation | async-start | bytes 65536 | tf_op jit(solution)/shard_map/all_to_all | solution.py:26
  84.6 8.8 %copy-start = (bf16[1,2048,256]{2,1,0:T(8,128)(2,1)S(1)}, bf16[1,2048,256]{2,1,0:T(8,128)(2,1)}, u32[]{:S(2)}) copy-start(bf16[1,2048,256]{2,1,0:T(8,128)(2,1)} %param.11) | copy-start | bytes 3145732
  84.6 11.2 %copy-start.1 = (bf16[1,2048,256]{2,1,0:T(8,128)(2,1)S(1)}, bf16[1,2048,256]{2,1,0:T(8,128)(2,1)}, u32[]{:S(2)}) copy-start(bf16[1,2048,256]{2,1,0:T(8,128)(2,1)} %param.12) | copy-start | bytes 3145732
  84.6 43.5 %copy-start.4 = (f32[1,512]{1,0:T(1,128)S(1)}, f32[1,512]{1,0:T(1,128)}, u32[]{:S(2)}) copy-start(f32[1,512]{1,0:T(1,128)} %param.9) | copy-start | bytes 6148
  84.6 43.6 %copy-start.3 = (s32[1,512]{1,0:T(1,128)S(1)}, s32[1,512]{1,0:T(1,128)}, u32[]{:S(2)}) copy-start(s32[1,512]{1,0:T(1,128)} %param.8) | copy-start | bytes 6148
  87.1 125.6 %all-to-all-start.1 = ((bf16[64,4,2048]{2,1,0:T(4,128)(2,1)}), bf16[64,4,2048]{2,1,0:T(4,128)(2,1)S(1)}, u32[]{:S(2)}, u32[]{:S(2)}) async-start(bf16[64,4,2048]{2,1,0:T(4,128)(2,1)} %reshape.181), calls=%async_computation.1 | async-start | bytes 2097152 | tf_op jit(solution)/shard_map/all_to_all | solution.py:26
  93.4 26.2 %collective-permute-start.3 = (bf16[2048,256]{1,0:T(8,128)(2,1)S(1)}, bf16[2048,256]{1,0:T(8,128)(2,1)S(1)}, u32[]{:S(2)}, u32[]{:S(2)}) collective-permute-start(bf16[2048,256]{1,0:T(8,128)(2,1)S(1)} %bitcast.43), channel_id=1, source_target_pairs={{0,1},{1,2},{2,3},{3,0},{4,5},{5,6},{6,7},{7,4},{8,9},{9,10},{10,1... | collective-permute-start | bytes 3145736 | tf_op jit(solution)/shard_map/ppermute | solution.py:14
  95.8 27.7 %collective-permute-start.7 = (bf16[2048,256]{1,0:T(8,128)(2,1)S(1)}, bf16[2048,256]{1,0:T(8,128)(2,1)S(1)}, u32[]{:S(2)}, u32[]{:S(2)}) collective-permute-start(bf16[2048,256]{1,0:T(8,128)(2,1)S(1)} %bitcast.46), channel_id=1, source_target_pairs={{0,3},{1,0},{2,1},{3,2},{4,7},{5,4},{6,5},{7,6},{8,11},{9,8},{10,9... | collective-permute-start | bytes 3145736 | tf_op jit(solution)/shard_map/ppermute | solution.py:14
  100.0 43.0 %collective-permute-start.4 = (bf16[2048,256]{1,0:T(8,128)(2,1)S(1)}, bf16[2048,256]{1,0:T(8,128)(2,1)S(1)}, u32[]{:S(2)}, u32[]{:S(2)}) collective-permute-start(bf16[2048,256]{1,0:T(8,128)(2,1)S(1)} %bitcast.44), channel_id=1, source_target_pairs={{0,3},{1,0},{2,1},{3,2},{4,7},{5,4},{6,5},{7,6},{8,11},{9,8},{10,9... | collective-permute-start | bytes 3145736 | tf_op jit(solution)/shard_map/ppermute | solution.py:14
  102.0 63.6 %collective-permute-start.10 = (bf16[256,2048]{1,0:T(8,128)(2,1)}, bf16[256,2048]{1,0:T(8,128)(2,1)S(1)}, u32[]{:S(2)}, u32[]{:S(2)}) collective-permute-start(bf16[256,2048]{1,0:T(8,128)(2,1)} %bitcast.49), channel_id=1, source_target_pairs={{0,3},{1,0},{2,1},{3,2},{4,7},{5,4},{6,5},{7,6},{8,11},{9,8},{10,9... | collective-permute-start | bytes 3145736 | tf_op jit(solution)/shard_map/ppermute | solution.py:14
  119.6 51.4 %collective-permute-start.5 = (bf16[2048,256]{1,0:T(8,128)(2,1)S(1)}, bf16[2048,256]{1,0:T(8,128)(2,1)S(1)}, u32[]{:S(2)}, u32[]{:S(2)}) collective-permute-start(bf16[2048,256]{1,0:T(8,128)(2,1)S(1)} %collective-permute-done.3), channel_id=1, source_target_pairs={{0,1},{1,2},{2,3},{3,0},{4,5},{5,6},{6,7},{7,4},{8,9},{9,10},{10,1... | collective-permute-start | bytes 3145736 | tf_op jit(solution)/shard_map/ppermute | solution.py:14
  121.6 51.8 %collective-permute-start.6 = (bf16[2048,256]{1,0:T(8,128)(2,1)S(1)}, bf16[2048,256]{1,0:T(8,128)(2,1)S(1)}, u32[]{:S(2)}, u32[]{:S(2)}) collective-permute-start(bf16[2048,256]{1,0:T(8,128)(2,1)S(1)} %bitcast.47), channel_id=1, source_target_pairs={{0,1},{1,2},{2,3},{3,0},{4,5},{5,6},{6,7},{7,4},{8,9},{9,10},{10,1... | collective-permute-start | bytes 3145736 | tf_op jit(solution)/shard_map/ppermute | solution.py:14
  123.5 64.4 %collective-permute-start.8 = (bf16[2048,256]{1,0:T(8,128)(2,1)S(1)}, bf16[2048,256]{1,0:T(8,128)(2,1)S(1)}, u32[]{:S(2)}, u32[]{:S(2)}) collective-permute-start(bf16[2048,256]{1,0:T(8,128)(2,1)S(1)} %collective-permute-done.7), channel_id=1, source_target_pairs={{0,3},{1,0},{2,1},{3,2},{4,7},{5,4},{6,5},{7,6},{8,11},{9,8},{10,9... | collective-permute-start | bytes 3145736 | tf_op jit(solution)/shard_map/ppermute | solution.py:14
  143.0 47.2 %collective-permute-start.9 = (bf16[256,2048]{1,0:T(8,128)(2,1)}, bf16[256,2048]{1,0:T(8,128)(2,1)S(1)}, u32[]{:S(2)}, u32[]{:S(2)}) collective-permute-start(bf16[256,2048]{1,0:T(8,128)(2,1)} %bitcast.50), channel_id=1, source_target_pairs={{0,1},{1,2},{2,3},{3,0},{4,5},{5,6},{6,7},{7,4},{8,9},{9,10},{10,1... | collective-permute-start | bytes 3145736 | tf_op jit(solution)/shard_map/ppermute | solution.py:14
  165.6 44.8 %collective-permute-start.11 = (bf16[256,2048]{1,0:T(8,128)(2,1)S(1)}, bf16[256,2048]{1,0:T(8,128)(2,1)S(1)}, u32[]{:S(2)}, u32[]{:S(2)}) collective-permute-start(bf16[256,2048]{1,0:T(8,128)(2,1)S(1)} %collective-permute-done.10), channel_id=1, source_target_pairs={{0,3},{1,0},{2,1},{3,2},{4,7},{5,4},{6,5},{7,6},{8,11},{9,8},{10,9... | collective-permute-start | bytes 3145736 | tf_op jit(solution)/shard_map/ppermute | solution.py:14
  173.3 37.1 %copy-start.2 = (bf16[1,256,2048]{2,1,0:T(8,128)(2,1)S(1)}, bf16[1,256,2048]{2,1,0:T(8,128)(2,1)}, u32[]{:S(2)}) copy-start(bf16[1,256,2048]{2,1,0:T(8,128)(2,1)} %param.13) | copy-start | bytes 3145732
  358.0 16.2 %all-to-all-start.3 = ((bf16[4,256,512]{2,1,0:T(8,128)(2,1)}), bf16[4,256,512]{2,1,0:T(8,128)(2,1)S(1)}, u32[]{:S(2)}, u32[]{:S(2)}) async-start(bf16[4,256,512]{2,1,0:T(8,128)(2,1)} %copy.26), calls=%async_computation.3 | async-start | bytes 2097152 | tf_op jit(solution)/shard_map/all_to_all | solution.py:106
